TPU v7x, 32 devices: a whole 2x2x4 slice. The times are simulated.
32 devices in a mesh: gx: 2 (over y), gy: 4 (over z), gz: 4 (over x, core).
Axes of the slice: x: 2, y: 2, z: 4, core: 2. Of those that a mesh axis runs over, the one named last changes fastest.
Arguments:
- node_latent: bfloat16 [2, 4, 4, 512, 128], P('gx', 'gy', 'gz'), may hold values from -6 to 6
- ghost_latent: bfloat16 [2, 4, 4, 6, 64, 128], P('gx', 'gy', 'gz'), may hold values from -6 to 6
- edge_latent: bfloat16 [2, 4, 4, 2816, 128], P('gx', 'gy', 'gz'), may hold values from -6 to 6
- senders: int32 [2, 4, 4, 2816], P('gx', 'gy', 'gz'), may hold values from 0 to 895
- receivers: int32 [2, 4, 4, 2816], P('gx', 'gy', 'gz'), may hold values from 0 to 511, never falling along the last dimension, each value on 1 to 12 neighbouring positions
- export_rows: int32 [2, 4, 4, 6, 64], P('gx', 'gy', 'gz'), may hold values from 0 to 512, as said below
- node_cotangent: bfloat16 [2, 4, 4, 512, 128], P('gx', 'gy', 'gz'), may hold values from -6 to 6
- edge_cotangent: bfloat16 [2, 4, 4, 2816, 128], P('gx', 'gy', 'gz'), may hold values from -6 to 6
- w_edge_in: bfloat16 [384, 128], replicated, may hold values from -0.3125 to 0.3125
- w_edge_hidden: bfloat16 [2, 128, 128], replicated, may hold values from -0.5 to 0.5
- b_edge: float32 [3, 128], replicated, may hold values from -3 to 3
- gain_edge: float32 [128], replicated, may hold values from 0.1 to 1.9
- shift_edge: float32 [128], replicated, may hold values from -3 to 3
- w_node_in: bfloat16 [256, 128], replicated, may hold values from -0.375 to 0.375
- w_node_hidden: bfloat16 [2, 128, 128], replicated, may hold values from -0.5 to 0.5
- b_node: float32 [3, 128], replicated, may hold values from -3 to 3
- gain_node: float32 [128], replicated, may hold values from 0.1 to 1.9
Outputs:
- node_grad: float32 [2, 4, 4, 512, 128], P('gx', 'gy', 'gz')
- edge_grad: bfloat16 [2, 4, 4, 2816, 128], P('gx', 'gy', 'gz')
- grad_w_edge_in: float32 [384, 128], replicated
- grad_w_edge_hidden: float32 [2, 128, 128], replicated
- grad_b_edge: float32 [3, 128], replicated
- grad_gain_edge: float32 [128], replicated
- grad_shift_edge: float32 [128], replicated
- grad_w_node_in: float32 [256, 128], replicated
- grad_w_node_hidden: float32 [2, 128, 128], replicated
- grad_b_node: float32 [3, 128], replicated
- grad_gain_node: float32 [128], replicated
Inputs may be any that keep to these rules, and one draw needn't show every extreme that they name: `export_rows`: for each block and face the leading slots hold distinct owned rows of that block; the remaining slots hold 512, marking an empty slot.
All inputs are finite; a program needn't handle non-finite values.
Results may differ from a plain program's by a relative error of at most 0.02.
Values sent between devices are 32-bit elements; how exact they have to be, the bound alone decides.
A program may use at most 64 MiB of HBM per device.

v0:
```python
import functools

import jax
import jax.numpy as jnp
from jax import lax
from jax.experimental import pallas as pl
from jax.experimental.pallas import tpu as pltpu
from jax.sharding import PartitionSpec as P

EPSILON = 1e-05
LANES = 128
FORWARD_TILES = 2
BACKWARD_TILES = 4
MESH = pl.DeviceIdType.MESH
AXES = ("gx", "gy", "gz")


def matmul(left, right):
    return jnp.dot(left, right, preferred_element_type=jnp.float32)


def matmul_nt(left, right):
    return lax.dot_general(
        left, right, (((1,), (1,)), ((), ())), preferred_element_type=jnp.float32
    )


def contract_rows(left, right):
    return lax.dot_general(
        left, right, (((0,), (0,)), ((), ())), preferred_element_type=jnp.float32
    )


def silu_parts(preact):
    sigmoid = 0.5 * jnp.tanh(0.5 * preact) + 0.5
    act = preact * sigmoid
    return act, sigmoid + act * (1.0 - sigmoid)


def norm_parts(preact):
    centred = preact - jnp.mean(preact, -1, keepdims=True)
    inv_std = lax.rsqrt(jnp.mean(centred * centred, -1, keepdims=True) + EPSILON)
    return centred * inv_std, inv_std


def norm_back(grad_out, gain, normed, inv_std):
    scaled = grad_out * gain
    return inv_std * (
        scaled
        - jnp.mean(scaled, -1, keepdims=True)
        - normed * jnp.mean(scaled * normed, -1, keepdims=True)
    )


def rows_sum(values):
    return jnp.sum(values, 0, keepdims=True)


def one_hot(hit):
    return jnp.where(hit, 1.0, 0.0).astype(jnp.bfloat16)


def stage_groups(sizes):
    near = [("gx", sizes["gx"], 1), ("gz", sizes["gz"], 1)]
    far = [("gy", sizes["gy"], 1)]
    return near, far


def group_size(group):
    count = 1
    for _, members, _ in group:
        count *= members
    return count


def coordinate(part):
    axis, count, stride = part
    return lax.rem(lax.axis_index(axis) // stride, count)


def member(group):
    index = 0
    for part in group:
        index = index * part[1] + coordinate(part)
    return index


def peers(group):
    steps = [()]
    for part in group:
        steps = [step + (more,) for step in steps for more in range(part[1])]
    found = []
    for step in steps[1:]:
        index = 0
        device = {}
        for part, more in zip(group, step):
            axis, count, stride = part
            mine = coordinate(part)
            other = lax.rem(mine + more, count)
            index = index * count + other
            here = device.get(axis, lax.axis_index(axis))
            device[axis] = here + (other - mine) * stride
        found.append((index, device))
    return found


class Reducer:
    def __init__(self, first, second, source, out, scratch):
        self.first, self.second = first, second
        self.source, self.out = source, out
        self.landing, self.swap, self.part = scratch[:3]
        self.sems = scratch[3:]
        self.piece = source.shape[0] // group_size(first)
        self.home = pl.ds(pl.multiple_of(member(first) * self.piece, 8), self.piece)
        self.pending = []

    def send(self, source, target, device, spot, stage):
        copy = pltpu.make_async_remote_copy(
            src_ref=source,
            dst_ref=target,
            send_sem=self.sems[2 * stage].at[spot],
            recv_sem=self.sems[2 * stage + 1].at[spot],
            device_id=device,
            device_id_type=MESH,
        )
        copy.start()
        self.pending.append(copy)

    def wait(self):
        for copy in self.pending:
            copy.wait()
        self.pending = []

    def scatter(self):
        for spot, (other, device) in enumerate(peers(self.first)):
            rows = pl.ds(pl.multiple_of(other * self.piece, 8), self.piece)
            self.send(self.source.at[rows], self.landing.at[spot], device, spot, 0)

    def exchange(self):
        self.wait()
        total = self.source[self.home]
        for spot in range(group_size(self.first) - 1):
            total = total + self.landing[spot]
        mine = member(self.second)
        self.part[...] = total
        self.swap[mine] = total
        for spot, (_, device) in enumerate(peers(self.second)):
            self.send(self.part, self.swap.at[mine], device, spot, 1)

    def gather(self):
        self.wait()
        total = self.swap[0]
        for index in range(1, group_size(self.second)):
            total = total + self.swap[index]
        self.out[self.home] = total
        for spot, (_, device) in enumerate(peers(self.first)):
            self.send(self.out.at[self.home], self.out.at[self.home], device, spot, 2)


def reducer_scratch(first, second, rows, width):
    one, two = group_size(first), group_size(second)
    piece = rows // one
    dma = pltpu.SemaphoreType.DMA
    return [
        pltpu.VMEM((one - 1, piece, width), jnp.float32),
        pltpu.VMEM((two, piece, width), jnp.float32),
        pltpu.VMEM((piece, width), jnp.float32),
        dma((one - 1,)),
        dma((one - 1,)),
        dma((two - 1,)),
        dma((two - 1,)),
        dma((one - 1,)),
        dma((one - 1,)),
    ]


def split_tiles(blocks, tiles):
    sizes = [blocks // tiles + (index < blocks % tiles) for index in range(tiles)]
    starts = [sum(sizes[:index]) for index in range(tiles)]
    return [(LANES * start, LANES * size) for start, size in zip(starts, sizes)]


def face_target(sizes, face):
    axis, side = AXES[face // 2], face % 2
    count = sizes[axis]
    step = 1 if side == 0 else count - 1
    return {axis: lax.rem(lax.axis_index(axis) + step, count)}


def block_kernel(
    sizes,
    edge_scale,
    node_scale,
    node,
    ghost,
    edge,
    snd,
    rcv,
    faces,
    ncot,
    ecot,
    we1,
    weh,
    be,
    ge,
    se,
    wn1,
    wnh,
    bn,
    gn,
    node_o,
    edge_o,
    nred_o,
    ared_o,
    bred_o,
    pick,
    put,
    table,
    z1_s,
    z2_s,
    r1_s,
    slope1_s,
    slope2_s,
    normed_s,
    inv_s,
    npack,
    apack,
    bpack,
    edge_s,
    ecot_s,
    ghost_s,
    halo,
    loads,
    hsend,
    hland,
    *scratch,
):
    nodes, width = node.shape
    edges = edge.shape[0]
    ghosts = ghost.shape[0]
    slots = ghosts // 6
    total = nodes + ghosts
    bf16, f32 = jnp.bfloat16, jnp.float32
    near, far = stage_groups(sizes)
    third = len(scratch) // 3
    node_red = Reducer(near, far, npack, nred_o, scratch[:third])
    a_red = Reducer(near, far, apack, ared_o, scratch[third : 2 * third])
    b_red = Reducer(far, near, bpack, bred_o, scratch[2 * third :])

    loaded = [
        pltpu.make_async_copy(edge, edge_s, loads.at[0]),
        pltpu.make_async_copy(ecot, ecot_s, loads.at[1]),
    ]
    for copy in loaded:
        copy.start()
    barrier = pltpu.get_barrier_semaphore()
    greeted = [face_target(sizes, face) for face in range(6)]
    for group in (near, far):
        greeted += [device for _, device in peers(group)]
    for device in greeted:
        pl.semaphore_signal(barrier, inc=1, device_id=device, device_id_type=MESH)

    lane = lax.broadcasted_iota(jnp.int32, (LANES, LANES), 1).astype(jnp.int16)
    sub = lax.broadcasted_iota(jnp.int32, (LANES, LANES), 0).astype(jnp.int16)
    one = jnp.ones((LANES, LANES), bf16)
    zero = jnp.zeros((LANES, LANES), bf16)

    def build(block, carry):
        at = pl.ds(pl.multiple_of(block * LANES, LANES), LANES)
        for ids, base, count in ((snd, 0, total), (rcv, total, nodes)):
            row = jnp.broadcast_to(ids[:, at], (LANES, LANES))
            column = jnp.transpose(row).astype(jnp.int16)
            row = row.astype(jnp.int16)
            for part in range(count // LANES):
                where = base + part * LANES
                pick[at, where : where + LANES] = jnp.where(
                    column == lane + jnp.int16(part * LANES), one, zero
                )
                put[where : where + LANES, at] = jnp.where(
                    row == sub + jnp.int16(part * LANES), one, zero
                )
        return carry

    lax.fori_loop(0, edges // LANES, build, 0)

    table[:nodes] = matmul(node[...], we1[width : 2 * width]).astype(bf16)
    table[nodes:total] = matmul(ghost[...], we1[width : 2 * width]).astype(bf16)
    table[total:] = matmul(node[...], we1[2 * width :]).astype(bf16)

    loaded[0].wait()
    agg = jnp.zeros((nodes, width), f32)
    for start, size in split_tiles(edges // LANES, FORWARD_TILES):
        at = pl.ds(start, size)
        first = matmul(edge_s[at], we1[:width]) + matmul(pick[at], table[...]) + be[0:1]
        act, slope = silu_parts(first)
        z1 = act.astype(bf16)
        z1_s[at] = z1
        slope1_s[at] = slope
        act, slope = silu_parts(matmul(z1, weh[0]) + be[1:2])
        z2 = act.astype(bf16)
        z2_s[at] = z2
        slope2_s[at] = slope
        normed, inv = norm_parts(matmul(z2, weh[1]) + be[2:3])
        normed_s[at] = normed
        inv_s[at] = jnp.broadcast_to(inv, normed.shape)
        new = (normed * ge[...] + se[...]).astype(bf16)
        agg = agg + matmul(put[total:, at], new)

    agg = agg.astype(bf16)
    first = matmul(node[...], wn1[:width]) + matmul(agg, wn1[width:]) + bn[0:1]
    act, slope1 = silu_parts(first)
    z1 = act.astype(bf16)
    act, slope2 = silu_parts(matmul(z1, wnh[0]) + bn[1:2])
    z2 = act.astype(bf16)
    normed, inv = norm_parts(matmul(z2, wnh[1]) + bn[2:3])
    up = ncot[...].astype(f32)
    gain_row = rows_sum(up * normed)
    g3 = norm_back(up, gn[...], normed, inv)
    r3 = g3.astype(bf16)
    g2 = matmul_nt(r3, wnh[1]) * slope2
    r2 = g2.astype(bf16)
    g1 = matmul_nt(r2, wnh[0]) * slope1
    r1 = g1.astype(bf16)
    node_o[...] = up + matmul_nt(r1, wn1[:width])
    agg_grad = matmul_nt(r1, wn1[width:]).astype(bf16)
    node_terms = [contract_rows(node[...], r1), contract_rows(agg, r1)]
    node_terms += [contract_rows(z1, r2), contract_rows(z2, r3)]
    for index, term in enumerate(node_terms):
        npack[index * width : (index + 1) * width] = term * node_scale
    for pack, used in ((npack, 4 * width), (apack, 4 * width), (bpack, width)):
        if pack.shape[0] > used:
            pack[used:] = jnp.zeros((pack.shape[0] - used, width), f32)
    for index, row in enumerate((rows_sum(g1), rows_sum(g2), rows_sum(g3), gain_row)):
        bpack[width + 5 + index : width + 6 + index] = row * node_scale

    pl.semaphore_wait(barrier, len(greeted))
    node_red.scatter()

    loaded[1].wait()
    small = [jnp.zeros((1, width), f32)] * 5
    acc = jnp.zeros((total + nodes, width), f32)
    grads = [jnp.zeros((width, width), f32)] * 3
    for number, (start, size) in enumerate(split_tiles(edges // LANES, BACKWARD_TILES)):
        at = pl.ds(start, size)
        up = ecot_s[at].astype(f32) + matmul(pick[at, total:], agg_grad)
        normed = normed_s[at]
        g3 = norm_back(up, ge[...], normed, inv_s[at])
        r3 = g3.astype(bf16)
        g2 = matmul_nt(r3, weh[1]) * slope2_s[at]
        r2 = g2.astype(bf16)
        g1 = matmul_nt(r2, weh[0]) * slope1_s[at]
        r1 = g1.astype(bf16)
        r1_s[at] = r1
        acc = acc + matmul(put[:, at], r1)
        grads[0] = grads[0] + contract_rows(edge_s[at], r1)
        grads[1] = grads[1] + contract_rows(z1_s[at], r2)
        grads[2] = grads[2] + contract_rows(z2_s[at], r3)
        for index, term in enumerate((g1, g2, g3, up * normed, up)):
            small[index] = small[index] + rows_sum(term)

    by_sender = acc[:total].astype(bf16)
    by_receiver = acc[total:].astype(bf16)
    middle = contract_rows(node[...], by_sender[:nodes])
    middle = middle + contract_rows(ghost[...], by_sender[nodes:])
    last = contract_rows(node[...], by_receiver)
    for index, term in enumerate((grads[0], middle, last, grads[1])):
        apack[index * width : (index + 1) * width] = term * edge_scale
    bpack[:width] = grads[2] * edge_scale
    for index, row in enumerate(small):
        bpack[width + index : width + 1 + index] = row * edge_scale
    a_red.scatter()
    b_red.scatter()
    node_red.exchange()

    full = matmul_nt(by_sender, we1[width : 2 * width])
    ghost_s[...] = full[nodes:]
    halos = []
    for face in range(6):
        rows = pl.ds(face * slots, slots)
        copy = pltpu.make_async_remote_copy(
            src_ref=ghost_s.at[rows],
            dst_ref=halo.at[rows],
            send_sem=hsend.at[face],
            recv_sem=hland.at[face],
            device_id=face_target(sizes, face),
            device_id_type=MESH,
        )
        copy.start()
        halos.append(copy)
    node_o[...] += full[:nodes] + matmul_nt(by_receiver, we1[2 * width :])
    half = edges // 2
    at = pl.ds(0, half)
    grad = ecot_s[at].astype(f32) + matmul_nt(r1_s[at], we1[:width])
    edge_o[at] = grad.astype(bf16)
    a_red.exchange()
    b_red.exchange()
    node_red.gather()
    at = pl.ds(half, edges - half)
    grad = ecot_s[at].astype(f32) + matmul_nt(r1_s[at], we1[:width])
    edge_o[at] = grad.astype(bf16)
    for copy in halos:
        copy.wait()
    spot = lax.broadcasted_iota(jnp.int32, (nodes, slots), 0)
    local = node_o[...]
    for face in range(6):
        values = halo[face * slots : (face + 1) * slots].astype(bf16)
        local = local + matmul(one_hot(spot == faces[face]), values)
    node_o[...] = local
    a_red.gather()
    b_red.gather()
    node_red.wait()
    a_red.wait()
    b_red.wait()


def finish_kernel(
    node, edge, nred, ared, bred, node_o, edge_o, we1_o, weh_o, be_o, ge_o, se_o, wn1_o, wnh_o, bn_o, gn_o
):
    width = node.shape[1]
    node_o[...] = node[...]
    edge_o[...] = edge[...]
    we1_o[...] = ared[: 3 * width]
    weh_o[0] = ared[3 * width : 4 * width]
    weh_o[1] = bred[:width]
    wn1_o[...] = nred[: 2 * width]
    wnh_o[0] = nred[2 * width : 3 * width]
    wnh_o[1] = nred[3 * width : 4 * width]
    be_o[...] = bred[width : width + 3]
    ge_o[...] = bred[width + 3 : width + 4]
    se_o[...] = bred[width + 4 : width + 5]
    bn_o[...] = bred[width + 5 : width + 8]
    gn_o[...] = bred[width + 8 : width + 9]


VMEM = pl.BlockSpec(memory_space=pltpu.VMEM)
HBM = pl.BlockSpec(memory_space=pl.ANY)


def on_device(
    sizes,
    node_latent,
    ghost_latent,
    edge_latent,
    senders,
    receivers,
    export_rows,
    node_cotangent,
    edge_cotangent,
    w_edge_in,
    w_edge_hidden,
    b_edge,
    gain_edge,
    shift_edge,
    w_node_in,
    w_node_hidden,
    b_node,
    gain_node,
):
    f32, bf16 = jnp.float32, jnp.bfloat16
    nodes, width = node_latent.shape[3:]
    slots = ghost_latent.shape[4]
    ghosts = 6 * slots
    edges = edge_latent.shape[3]
    total = nodes + ghosts
    devices = sizes["gx"] * sizes["gy"] * sizes["gz"]
    edge_scale = float(edges * devices) ** (-0.5)
    node_scale = float(nodes * devices) ** (-0.5)

    def padded(rows, group):
        unit = 8 * group_size(group)
        return -(-rows // unit) * unit

    def shape(*dims, dtype=f32):
        return jax.ShapeDtypeStruct(dims, dtype)

    near, far = stage_groups(sizes)
    four, two = padded(4 * width, near), padded(width + 9, far)
    reducers = reducer_scratch(near, far, four, width)
    reducers += reducer_scratch(near, far, four, width)
    reducers += reducer_scratch(far, near, two, width)
    passed = pl.pallas_call(
        functools.partial(block_kernel, sizes, edge_scale, node_scale),
        out_shape=(
            shape(nodes, width),
            shape(edges, width, dtype=bf16),
            shape(four, width),
            shape(four, width),
            shape(two, width),
        ),
        in_specs=[VMEM] * 2 + [HBM] + [VMEM] * 4 + [HBM] + [VMEM] * 9,
        out_specs=(VMEM,) * 5,
        scratch_shapes=[
            pltpu.VMEM((edges, total + nodes), bf16),
            pltpu.VMEM((total + nodes, edges), bf16),
            pltpu.VMEM((total + nodes, width), bf16),
            pltpu.VMEM((edges, width), bf16),
            pltpu.VMEM((edges, width), bf16),
            pltpu.VMEM((edges, width), bf16),
            pltpu.VMEM((edges, width), f32),
            pltpu.VMEM((edges, width), f32),
            pltpu.VMEM((edges, width), f32),
            pltpu.VMEM((edges, width), f32),
            pltpu.VMEM((four, width), f32),
            pltpu.VMEM((four, width), f32),
            pltpu.VMEM((two, width), f32),
            pltpu.VMEM((edges, width), bf16),
            pltpu.VMEM((edges, width), bf16),
            pltpu.VMEM((ghosts, width), f32),
            pltpu.VMEM((ghosts, width), f32),
            pltpu.SemaphoreType.DMA((2,)),
            pltpu.SemaphoreType.DMA((6,)),
            pltpu.SemaphoreType.DMA((6,)),
        ]
        + reducers,
        compiler_params=pltpu.CompilerParams(
            collective_id=0, has_side_effects=True, vmem_limit_bytes=60 * 1024 * 1024
        ),
        name="block_pass",
    )(
        node_latent.reshape(nodes, width),
        ghost_latent.reshape(ghosts, width),
        edge_latent.reshape(edges, width),
        senders.reshape(1, edges),
        receivers.reshape(1, edges),
        export_rows.reshape(6, 1, slots),
        node_cotangent.reshape(nodes, width),
        edge_cotangent.reshape(edges, width),
        w_edge_in,
        w_edge_hidden,
        b_edge,
        gain_edge.reshape(1, width),
        shift_edge.reshape(1, width),
        w_node_in,
        w_node_hidden,
        b_node,
        gain_node.reshape(1, width),
    )

    outs = pl.pallas_call(
        finish_kernel,
        out_shape=(
            shape(nodes, width),
            shape(edges, width, dtype=bf16),
            shape(3 * width, width),
            shape(2, width, width),
            shape(3, width),
            shape(1, width),
            shape(1, width),
            shape(2 * width, width),
            shape(2, width, width),
            shape(3, width),
            shape(1, width),
        ),
        in_specs=[VMEM] * 5,
        out_specs=(VMEM,) * 11,
        name="finish",
    )(*passed)
    node_grad, edge_grad, we1, weh, be, ge, se, wn1, wnh, bn, gn = outs
    return (
        node_grad.reshape(node_latent.shape),
        edge_grad.reshape(edge_latent.shape),
        we1,
        weh,
        be,
        ge.reshape(width),
        se.reshape(width),
        wn1,
        wnh,
        bn,
        gn.reshape(width),
    )


def solution(mesh):
    block = P("gx", "gy", "gz")
    sizes = dict(mesh.shape)
    return jax.shard_map(
        functools.partial(on_device, sizes),
        mesh=mesh,
        in_specs=(block,) * 8 + (P(),) * 9,
        out_specs=(block,) * 2 + (P(),) * 9,
        check_vma=False,
    )
```

profile of v0, /device:TPU:0, one launch (start us, length us, event | category | flops | bytes accessed | tf_op | source)
XLA Modules:
  0.0 40.5 jit_solution(17029419554173345392)
XLA Ops:
  0.7 37.3 %block_pass.1 = (f32[512,128]{1,0:T(8,128)}, bf16[2816,128]{1,0:T(8,128)(2,1)}, f32[512,128]{1,0:T(8,128)}, f32[512,128]{1,0:T(8,128)}, f32[160,128]{1,0:T(8,128)}) custom-call(bf16[512,128]{1,0:T(8,128)(2,1)} %bitcast.18, bf16[384,128]{1,0:T(8,128)(2,1)} %bitcast.20, bf16[2816,128]{1,0:T(8,128)(2,1)} %bitcast.16, s32[1,2816]{1,0:T(1,128)} %bitcast.21, ...), custom_call_target="tpu_custom_call" | custom-call | tf_op jit(solution)/shard_map/block_pass/pallas_call | solution.py:481
  37.9 2.5 %finish.1 = (f32[512,128]{1,0:T(8,128)}, bf16[2816,128]{1,0:T(8,128)(2,1)}, f32[384,128]{1,0:T(8,128)}, f32[2,128,128]{2,1,0:T(8,128)}, f32[3,128]{1,0:T(4,128)}...) custom-call(f32[512,128]{1,0:T(8,128)} %get-tuple-element.27.node, ...), custom_call_target="tpu_custom_call" | custom-call | tf_op jit(solution)/shard_map/finish/pallas_call | solution.py:539
where the time goes:
time: 40.6 us; the launch traced here: 40.5 us
  Pallas kernels  39.8 us (98%)
  between operations  0.66 us (2%)
    pallas_call x1, Pallas kernels, on_device(): pl.pallas_call(functools.partial(block_kernel, sizes, edge_scale, node_sc...  37.3 us
    pallas_call x1, Pallas kernels, on_device(): pl.pallas_call(finish_kernel, out_shape=(shape(nodes, width), shape(edges...  2.54 us

commit v1 on v0

--- a/solution.py
+++ b/solution.py
@@ -9,8 +9,8 @@
 
 EPSILON = 1e-05
 LANES = 128
-FORWARD_TILES = 2
-BACKWARD_TILES = 4
+FORWARD_TILE = 512
+BACKWARD_TILE = 512
 MESH = pl.DeviceIdType.MESH
 AXES = ("gx", "gy", "gz")
 
@@ -31,24 +31,24 @@
     )
 
 
-def silu_parts(preact):
-    sigmoid = 0.5 * jnp.tanh(0.5 * preact) + 0.5
-    act = preact * sigmoid
-    return act, sigmoid + act * (1.0 - sigmoid)
+def silu_parts(half):
+    th = jnp.tanh(half)
+    lifted = 1.0 + th
+    act = half * lifted
+    return act, lifted + act * (1.0 - th)
 
 
 def norm_parts(preact):
-    centred = preact - jnp.mean(preact, -1, keepdims=True)
-    inv_std = lax.rsqrt(jnp.mean(centred * centred, -1, keepdims=True) + EPSILON)
+    centred = preact - jnp.mean(preact, 0, keepdims=True)
+    inv_std = lax.rsqrt(jnp.mean(centred * centred, 0, keepdims=True) + EPSILON)
     return centred * inv_std, inv_std
 
 
-def norm_back(grad_out, gain, normed, inv_std):
-    scaled = grad_out * gain
+def norm_back(scaled, normed, inv_std):
     return inv_std * (
         scaled
-        - jnp.mean(scaled, -1, keepdims=True)
-        - normed * jnp.mean(scaled * normed, -1, keepdims=True)
+        - jnp.mean(scaled, 0, keepdims=True)
+        - normed * jnp.mean(scaled * normed, 0, keepdims=True)
     )
 
 
@@ -58,6 +58,27 @@
 
 def one_hot(hit):
     return jnp.where(hit, 1.0, 0.0).astype(jnp.bfloat16)
+
+
+def wide(column, lanes):
+    return jnp.concatenate([column] * (lanes // LANES), 1)
+
+
+def lane_fold(values):
+    total = values[:, :LANES]
+    for start in range(LANES, values.shape[1], LANES):
+        total = total + values[:, start : start + LANES]
+    return total
+
+
+def chain(lefts, rights):
+    total = None
+    for start in range(0, len(lefts), 2):
+        left = jnp.concatenate(lefts[start : start + 2], 1)
+        right = jnp.concatenate(rights[start : start + 2], 0)
+        term = matmul(left, right)
+        total = term if total is None else total + term
+    return total
 
 
 def stage_groups(sizes):
@@ -174,10 +195,8 @@
     ]
 
 
-def split_tiles(blocks, tiles):
-    sizes = [blocks // tiles + (index < blocks % tiles) for index in range(tiles)]
-    starts = [sum(sizes[:index]) for index in range(tiles)]
-    return [(LANES * start, LANES * size) for start, size in zip(starts, sizes)]
+def tiles(rows, size):
+    return [(start, min(size, rows - start)) for start in range(0, rows, size)]
 
 
 def face_target(sizes, face):
@@ -213,8 +232,9 @@
     nred_o,
     ared_o,
     bred_o,
-    pick,
-    put,
+    node_id,
+    snd_col,
+    rcv_col,
     table,
     z1_s,
     z2_s,
@@ -261,119 +281,170 @@
         pl.semaphore_signal(barrier, inc=1, device_id=device, device_id_type=MESH)
 
     lane = lax.broadcasted_iota(jnp.int32, (LANES, LANES), 1).astype(jnp.int16)
-    sub = lax.broadcasted_iota(jnp.int32, (LANES, LANES), 0).astype(jnp.int16)
+    sub = lax.broadcasted_iota(jnp.int32, (LANES, LANES), 0)
     one = jnp.ones((LANES, LANES), bf16)
     zero = jnp.zeros((LANES, LANES), bf16)
-
-    def build(block, carry):
-        at = pl.ds(pl.multiple_of(block * LANES, LANES), LANES)
-        for ids, base, count in ((snd, 0, total), (rcv, total, nodes)):
-            row = jnp.broadcast_to(ids[:, at], (LANES, LANES))
-            column = jnp.transpose(row).astype(jnp.int16)
-            row = row.astype(jnp.int16)
-            for part in range(count // LANES):
-                where = base + part * LANES
-                pick[at, where : where + LANES] = jnp.where(
-                    column == lane + jnp.int16(part * LANES), one, zero
-                )
-                put[where : where + LANES, at] = jnp.where(
-                    row == sub + jnp.int16(part * LANES), one, zero
-                )
-        return carry
-
-    lax.fori_loop(0, edges // LANES, build, 0)
-
-    table[:nodes] = matmul(node[...], we1[width : 2 * width]).astype(bf16)
-    table[nodes:total] = matmul(ghost[...], we1[width : 2 * width]).astype(bf16)
-    table[total:] = matmul(node[...], we1[2 * width :]).astype(bf16)
+    for part in range(total // LANES):
+        node_id[part] = (sub + part * LANES).astype(jnp.int16)
+
+    def column(row):
+        return jnp.transpose(jnp.broadcast_to(row, (LANES, LANES)))
+
+    for block in range(edges // LANES):
+        at = slice(block * LANES, (block + 1) * LANES)
+        snd_col[block] = column(snd[:, at]).astype(jnp.int16)
+        rcv_col[block] = column(rcv[:, at]).astype(jnp.int16)
+
+    def node_hots(ids, start, size, count):
+        rows = [
+            jnp.broadcast_to(ids[:, spot : spot + LANES], (LANES, LANES)).astype(jnp.int16)
+            for spot in range(start, start + size, LANES)
+        ]
+        return [
+            jnp.concatenate([jnp.where(row == node_id[part], one, zero) for row in rows], 1)
+            for part in range(count // LANES)
+        ]
+
+    def edge_hots(columns, block, first, count):
+        ids = columns[block]
+        return jnp.concatenate(
+            [
+                jnp.where(ids == lane + jnp.int16(part * LANES), one, zero)
+                for part in range(first // LANES, (first + count) // LANES)
+            ],
+            1,
+        )
+
+    def blocks_of(ref, start, size):
+        spots = range(start // LANES, (start + size) // LANES)
+        return jnp.concatenate([ref[spot] for spot in spots], 1)
+
+    def put_blocks(ref, start, values):
+        for spot in range(values.shape[1] // LANES):
+            ref[start // LANES + spot] = values[:, spot * LANES : (spot + 1) * LANES]
+
+    half = jnp.bfloat16(0.5)
+    half_t = lambda weight: jnp.transpose(weight * half)
+    w1 = [half_t(we1[index * width : (index + 1) * width]) for index in range(3)]
+    w2, w3 = half_t(weh[0]), jnp.transpose(weh[1])
+    back3, back2 = weh[1] * half, weh[0] * half
+    bias = [column(0.5 * be[0:1]), column(0.5 * be[1:2]), column(be[2:3])]
+    gain, shift = column(ge[...]), column(se[...])
+
+    put_blocks(table, 0, matmul_nt(w1[1], node[...]).astype(bf16))
+    put_blocks(table, nodes, matmul_nt(w1[1], ghost[...]).astype(bf16))
+    put_blocks(table, total, matmul_nt(w1[2], node[...]).astype(bf16))
+    spots = (total + nodes) // LANES
 
     loaded[0].wait()
-    agg = jnp.zeros((nodes, width), f32)
-    for start, size in split_tiles(edges // LANES, FORWARD_TILES):
+    agg = None
+    for start, size in tiles(edges, FORWARD_TILE):
         at = pl.ds(start, size)
-        first = matmul(edge_s[at], we1[:width]) + matmul(pick[at], table[...]) + be[0:1]
-        act, slope = silu_parts(first)
+        rights = [jnp.transpose(edge_s[at])]
+        rights += node_hots(snd, start, size, total) + node_hots(rcv, start, size, nodes)
+        first = chain([w1[0]] + [table[spot] for spot in range(spots)], rights)
+        act, slope = silu_parts(first + wide(bias[0], size))
         z1 = act.astype(bf16)
-        z1_s[at] = z1
-        slope1_s[at] = slope
-        act, slope = silu_parts(matmul(z1, weh[0]) + be[1:2])
+        put_blocks(z1_s, start, z1)
+        put_blocks(slope1_s, start, slope)
+        act, slope = silu_parts(matmul(w2, z1) + wide(bias[1], size))
         z2 = act.astype(bf16)
-        z2_s[at] = z2
-        slope2_s[at] = slope
-        normed, inv = norm_parts(matmul(z2, weh[1]) + be[2:3])
-        normed_s[at] = normed
-        inv_s[at] = jnp.broadcast_to(inv, normed.shape)
-        new = (normed * ge[...] + se[...]).astype(bf16)
-        agg = agg + matmul(put[total:, at], new)
+        put_blocks(z2_s, start, z2)
+        put_blocks(slope2_s, start, slope)
+        normed, inv = norm_parts(matmul(w3, z2) + wide(bias[2], size))
+        put_blocks(normed_s, start, normed)
+        put_blocks(inv_s, start, inv)
+        new = (normed * wide(gain, size) + wide(shift, size)).astype(bf16)
+        lefts = [new[:, spot : spot + LANES] for spot in range(0, size, LANES)]
+        rights = [edge_hots(rcv_col, (start + spot) // LANES, 0, nodes) for spot in range(0, size, LANES)]
+        term = chain(lefts, rights)
+        agg = term if agg is None else agg + term
 
     agg = agg.astype(bf16)
-    first = matmul(node[...], wn1[:width]) + matmul(agg, wn1[width:]) + bn[0:1]
-    act, slope1 = silu_parts(first)
+    n1a, n1b = half_t(wn1[:width]), half_t(wn1[width:])
+    n2, n3 = half_t(wnh[0]), jnp.transpose(wnh[1])
+    first = matmul_nt(n1a, node[...]) + matmul(n1b, agg)
+    act, slope1 = silu_parts(first + wide(column(0.5 * bn[0:1]), nodes))
     z1 = act.astype(bf16)
-    act, slope2 = silu_parts(matmul(z1, wnh[0]) + bn[1:2])
+    act, slope2 = silu_parts(matmul(n2, z1) + wide(column(0.5 * bn[1:2]), nodes))
     z2 = act.astype(bf16)
-    normed, inv = norm_parts(matmul(z2, wnh[1]) + bn[2:3])
-    up = ncot[...].astype(f32)
-    gain_row = rows_sum(up * normed)
-    g3 = norm_back(up, gn[...], normed, inv)
+    normed, inv = norm_parts(matmul(n3, z2) + wide(column(bn[2:3]), nodes))
+    up = jnp.transpose(ncot[...]).astype(f32)
+    gain_sum = lane_fold(up * normed)
+    g3 = norm_back(up * wide(column(gn[...]), nodes), normed, inv)
     r3 = g3.astype(bf16)
-    g2 = matmul_nt(r3, wnh[1]) * slope2
+    g2 = matmul(wnh[1] * half, r3) * slope2
     r2 = g2.astype(bf16)
-    g1 = matmul_nt(r2, wnh[0]) * slope1
+    g1 = matmul(wnh[0] * half, r2) * slope1
     r1 = g1.astype(bf16)
-    node_o[...] = up + matmul_nt(r1, wn1[:width])
-    agg_grad = matmul_nt(r1, wn1[width:]).astype(bf16)
-    node_terms = [contract_rows(node[...], r1), contract_rows(agg, r1)]
-    node_terms += [contract_rows(z1, r2), contract_rows(z2, r3)]
+    agg_grad = matmul(wn1[width:], r1).astype(bf16)
+    node_part = up + matmul(wn1[:width], r1)
+    node_terms = [jnp.transpose(matmul(r1, node[...])), matmul_nt(agg, r1)]
+    node_terms += [matmul_nt(z1, r2), matmul_nt(z2, r3)]
     for index, term in enumerate(node_terms):
         npack[index * width : (index + 1) * width] = term * node_scale
     for pack, used in ((npack, 4 * width), (apack, 4 * width), (bpack, width)):
         if pack.shape[0] > used:
             pack[used:] = jnp.zeros((pack.shape[0] - used, width), f32)
-    for index, row in enumerate((rows_sum(g1), rows_sum(g2), rows_sum(g3), gain_row)):
-        bpack[width + 5 + index : width + 6 + index] = row * node_scale
+
+    def row_of(folded):
+        return rows_sum(jnp.transpose(folded))
+
+    node_sums = (lane_fold(g1), lane_fold(g2), lane_fold(g3), gain_sum)
+    for index, value in enumerate(node_sums):
+        bpack[width + 5 + index : width + 6 + index] = row_of(value) * node_scale
 
     pl.semaphore_wait(barrier, len(greeted))
     node_red.scatter()
 
     loaded[1].wait()
-    small = [jnp.zeros((1, width), f32)] * 5
-    acc = jnp.zeros((total + nodes, width), f32)
-    grads = [jnp.zeros((width, width), f32)] * 3
-    for number, (start, size) in enumerate(split_tiles(edges // LANES, BACKWARD_TILES)):
+    small = [None] * 5
+    grads = [None] * 3
+    more = lambda old, new: new if old is None else old + new
+    lefts = [agg_grad[:, spot : spot + LANES] for spot in range(0, nodes, LANES)]
+    for start, size in tiles(edges, BACKWARD_TILE):
         at = pl.ds(start, size)
-        up = ecot_s[at].astype(f32) + matmul(pick[at, total:], agg_grad)
-        normed = normed_s[at]
-        g3 = norm_back(up, ge[...], normed, inv_s[at])
+        up = jnp.transpose(ecot_s[at]).astype(f32)
+        up = up + chain(lefts, node_hots(rcv, start, size, nodes))
+        normed = blocks_of(normed_s, start, size)
+        g3 = norm_back(up * wide(gain, size), normed, blocks_of(inv_s, start, size))
         r3 = g3.astype(bf16)
-        g2 = matmul_nt(r3, weh[1]) * slope2_s[at]
+        g2 = matmul(back3, r3) * blocks_of(slope2_s, start, size)
         r2 = g2.astype(bf16)
-        g1 = matmul_nt(r2, weh[0]) * slope1_s[at]
+        g1 = matmul(back2, r2) * blocks_of(slope1_s, start, size)
         r1 = g1.astype(bf16)
-        r1_s[at] = r1
-        acc = acc + matmul(put[:, at], r1)
-        grads[0] = grads[0] + contract_rows(edge_s[at], r1)
-        grads[1] = grads[1] + contract_rows(z1_s[at], r2)
-        grads[2] = grads[2] + contract_rows(z2_s[at], r3)
+        put_blocks(r1_s, start, r1)
+        grads[0] = more(grads[0], matmul(r1, edge_s[at]))
+        grads[1] = more(grads[1], matmul_nt(blocks_of(z1_s, start, size), r2))
+        grads[2] = more(grads[2], matmul_nt(blocks_of(z2_s, start, size), r3))
         for index, term in enumerate((g1, g2, g3, up * normed, up)):
-            small[index] = small[index] + rows_sum(term)
-
-    by_sender = acc[:total].astype(bf16)
-    by_receiver = acc[total:].astype(bf16)
-    middle = contract_rows(node[...], by_sender[:nodes])
-    middle = middle + contract_rows(ghost[...], by_sender[nodes:])
-    last = contract_rows(node[...], by_receiver)
-    for index, term in enumerate((grads[0], middle, last, grads[1])):
+            small[index] = more(small[index], lane_fold(term))
+
+    lefts = [r1_s[block] for block in range(edges // LANES)]
+    by_sender = []
+    for start, size in tiles(total, 2 * LANES):
+        rights = [edge_hots(snd_col, block, start, size) for block in range(edges // LANES)]
+        by_sender.append(chain(lefts, rights).astype(bf16))
+    by_receiver = []
+    for start, size in tiles(nodes, 2 * LANES):
+        rights = [edge_hots(rcv_col, block, start, size) for block in range(edges // LANES)]
+        by_receiver.append(chain(lefts, rights).astype(bf16))
+    by_sender = jnp.concatenate(by_sender, 1)
+    by_receiver = jnp.concatenate(by_receiver, 1)
+    middle = matmul(by_sender[:, :nodes], node[...]) + matmul(by_sender[:, nodes:], ghost[...])
+    last = matmul(by_receiver, node[...])
+    turned = [jnp.transpose(term) for term in (grads[0], middle, last)]
+    for index, term in enumerate(turned + [grads[1]]):
         apack[index * width : (index + 1) * width] = term * edge_scale
     bpack[:width] = grads[2] * edge_scale
-    for index, row in enumerate(small):
-        bpack[width + index : width + 1 + index] = row * edge_scale
+    for index, value in enumerate(small):
+        bpack[width + index : width + 1 + index] = row_of(value) * edge_scale
     a_red.scatter()
     b_red.scatter()
     node_red.exchange()
 
-    full = matmul_nt(by_sender, we1[width : 2 * width])
-    ghost_s[...] = full[nodes:]
+    full = matmul(we1[width : 2 * width], by_sender)
+    ghost_s[...] = jnp.transpose(full[:, nodes:])
     halos = []
     for face in range(6):
         rows = pl.ds(face * slots, slots)
@@ -387,17 +458,21 @@
         )
         copy.start()
         halos.append(copy)
-    node_o[...] += full[:nodes] + matmul_nt(by_receiver, we1[2 * width :])
-    half = edges // 2
-    at = pl.ds(0, half)
-    grad = ecot_s[at].astype(f32) + matmul_nt(r1_s[at], we1[:width])
-    edge_o[at] = grad.astype(bf16)
+    node_part = node_part + full[:, :nodes] + matmul(we1[2 * width :], by_receiver)
+    node_o[...] = jnp.transpose(node_part)
+
+    def edge_out(first, last):
+        for block in range(first, last):
+            at = pl.ds(block * LANES, LANES)
+            grad = ecot_s[at].astype(f32) + matmul_nt(jnp.transpose(r1_s[block]), we1[:width])
+            edge_o[at] = grad.astype(bf16)
+
+    middle_block = edges // LANES // 2
+    edge_out(0, middle_block)
     a_red.exchange()
     b_red.exchange()
     node_red.gather()
-    at = pl.ds(half, edges - half)
-    grad = ecot_s[at].astype(f32) + matmul_nt(r1_s[at], we1[:width])
-    edge_o[at] = grad.astype(bf16)
+    edge_out(middle_block, edges // LANES)
     for copy in halos:
         copy.wait()
     spot = lax.broadcasted_iota(jnp.int32, (nodes, slots), 0)
@@ -490,16 +565,17 @@
         in_specs=[VMEM] * 2 + [HBM] + [VMEM] * 4 + [HBM] + [VMEM] * 9,
         out_specs=(VMEM,) * 5,
         scratch_shapes=[
-            pltpu.VMEM((edges, total + nodes), bf16),
-            pltpu.VMEM((total + nodes, edges), bf16),
-            pltpu.VMEM((total + nodes, width), bf16),
-            pltpu.VMEM((edges, width), bf16),
-            pltpu.VMEM((edges, width), bf16),
-            pltpu.VMEM((edges, width), bf16),
-            pltpu.VMEM((edges, width), f32),
-            pltpu.VMEM((edges, width), f32),
-            pltpu.VMEM((edges, width), f32),
-            pltpu.VMEM((edges, width), f32),
+            pltpu.VMEM((total // LANES, LANES, LANES), jnp.int16),
+            pltpu.VMEM((edges // LANES, LANES, LANES), jnp.int16),
+            pltpu.VMEM((edges // LANES, LANES, LANES), jnp.int16),
+            pltpu.VMEM(((total + nodes) // LANES, LANES, LANES), bf16),
+            pltpu.VMEM((edges // LANES, LANES, LANES), bf16),
+            pltpu.VMEM((edges // LANES, LANES, LANES), bf16),
+            pltpu.VMEM((edges // LANES, LANES, LANES), bf16),
+            pltpu.VMEM((edges // LANES, LANES, LANES), f32),
+            pltpu.VMEM((edges // LANES, LANES, LANES), f32),
+            pltpu.VMEM((edges // LANES, LANES, LANES), f32),
+            pltpu.VMEM((edges // LANES, 1, LANES), f32),
             pltpu.VMEM((four, width), f32),
             pltpu.VMEM((four, width), f32),
             pltpu.VMEM((two, width), f32),

time: 40.6 us -> 38.4 us (0.946)
  Pallas kernels: 39.8 us -> 37.6 us
    pallas_call x1, Pallas kernels: 37.3 us -> 35.1 us  [on_device(): pl.pallas_call(functools.partial(block_kernel, sizes, edge_scale, node_sc...]
where the time goes in v1:
time: 38.4 us; the launch traced here: 38.3 us
  Pallas kernels  37.6 us (98%)
  between operations  0.66 us (2%)
    pallas_call x1, Pallas kernels, on_device(): pl.pallas_call(functools.partial(block_kernel, sizes, edge_scale, node_sc...  35.1 us
    pallas_call x1, Pallas kernels, on_device(): pl.pallas_call(finish_kernel, out_shape=(shape(nodes, width), shape(edges...  2.54 us

profile of v1, /device:TPU:0, one launch (start us, length us, event | category | flops | bytes accessed | tf_op | source)
XLA Modules:
  0.0 38.3 jit_solution(14890689018474334149)
XLA Ops:
  0.7 35.1 %block_pass.1 = (f32[512,128]{1,0:T(8,128)}, bf16[2816,128]{1,0:T(8,128)(2,1)}, f32[512,128]{1,0:T(8,128)}, f32[512,128]{1,0:T(8,128)}, f32[160,128]{1,0:T(8,128)}) custom-call(bf16[512,128]{1,0:T(8,128)(2,1)} %bitcast.18, bf16[384,128]{1,0:T(8,128)(2,1)} %bitcast.20, bf16[2816,128]{1,0:T(8,128)(2,1)} %bitcast.16, s32[1,2816]{1,0:T(1,128)} %bitcast.21, ...), custom_call_target="tpu_custom_call" | custom-call | tf_op jit(solution)/shard_map/block_pass/pallas_call | solution.py:556
  35.7 2.5 %finish.1 = (f32[512,128]{1,0:T(8,128)}, bf16[2816,128]{1,0:T(8,128)(2,1)}, f32[384,128]{1,0:T(8,128)}, f32[2,128,128]{2,1,0:T(8,128)}, f32[3,128]{1,0:T(4,128)}...) custom-call(f32[512,128]{1,0:T(8,128)} %get-tuple-element.27.node, ...), custom_call_target="tpu_custom_call" | custom-call | tf_op jit(solution)/shard_map/finish/pallas_call | solution.py:615

commit v2 on v1

--- a/solution.py
+++ b/solution.py
@@ -9,8 +9,8 @@
 
 EPSILON = 1e-05
 LANES = 128
-FORWARD_TILE = 512
-BACKWARD_TILE = 512
+FORWARD_TILE = 1408
+BACKWARD_TILE = 1408
 MESH = pl.DeviceIdType.MESH
 AXES = ("gx", "gy", "gz")
 
@@ -82,9 +82,12 @@
 
 
 def stage_groups(sizes):
+    pair = 2 if sizes["gz"] % 2 == 0 else 1
+    core = [("gz", pair, 1)]
+    chips = [("gx", sizes["gx"], 1), ("gz", sizes["gz"] // pair, pair)]
     near = [("gx", sizes["gx"], 1), ("gz", sizes["gz"], 1)]
     far = [("gy", sizes["gy"], 1)]
-    return near, far
+    return core, chips, near, far
 
 
 def group_size(group):
@@ -126,21 +129,26 @@
 
 
 class Reducer:
-    def __init__(self, first, second, source, out, scratch):
-        self.first, self.second = first, second
-        self.source, self.out = source, out
-        self.landing, self.swap, self.part = scratch[:3]
-        self.sems = scratch[3:]
-        self.piece = source.shape[0] // group_size(first)
-        self.home = pl.ds(pl.multiple_of(member(first) * self.piece, 8), self.piece)
+    def __init__(self, groups, last, source, out, scratch):
+        self.groups, self.last, self.source, self.out = groups, last, source, out
+        self.scratch = list(scratch)
+        self.now, self.spot, self.rows = source, 0, source.shape[0]
+        self.homes = []
         self.pending = []
-
-    def send(self, source, target, device, spot, stage):
+        self.steps = [functools.partial(self.scatter, group) for group in groups]
+        self.steps += [self.exchange, self.settle]
+        self.steps += [functools.partial(self.gather, group) for group in groups[-2::-1]]
+        self.steps += [self.wait]
+
+    def advance(self):
+        self.steps.pop(0)()
+
+    def send(self, source, target, device, spot, sems):
         copy = pltpu.make_async_remote_copy(
             src_ref=source,
             dst_ref=target,
-            send_sem=self.sems[2 * stage].at[spot],
-            recv_sem=self.sems[2 * stage + 1].at[spot],
+            send_sem=sems[0].at[spot],
+            recv_sem=sems[1].at[spot],
             device_id=device,
             device_id_type=MESH,
         )
@@ -152,47 +160,74 @@
             copy.wait()
         self.pending = []
 
-    def scatter(self):
-        for spot, (other, device) in enumerate(peers(self.first)):
-            rows = pl.ds(pl.multiple_of(other * self.piece, 8), self.piece)
-            self.send(self.source.at[rows], self.landing.at[spot], device, spot, 0)
+    def fold(self):
+        if not self.homes:
+            return
+        self.wait()
+        landing, part, own = self.arrived
+        total = own[...]
+        for spot in range(self.count):
+            total = total + landing[spot]
+        part[...] = total
+        self.now = part
+
+    def scatter(self, group):
+        self.fold()
+        landing, part, *sems = self.scratch[:4]
+        self.scratch = self.scratch[4:]
+        piece = self.now.shape[0] // group_size(group)
+        for spot, (other, device) in enumerate(peers(group)):
+            rows = pl.ds(pl.multiple_of(other * piece, 8), piece)
+            self.send(self.now.at[rows], landing.at[spot], device, spot, sems)
+        self.count = group_size(group) - 1
+        mine = member(group) * piece
+        self.spot = self.spot + mine
+        self.homes.append((self.spot, piece))
+        self.arrived = landing, part, self.now.at[pl.ds(pl.multiple_of(mine, 8), piece)]
 
     def exchange(self):
-        self.wait()
-        total = self.source[self.home]
-        for spot in range(group_size(self.first) - 1):
-            total = total + self.landing[spot]
-        mine = member(self.second)
-        self.part[...] = total
-        self.swap[mine] = total
-        for spot, (_, device) in enumerate(peers(self.second)):
-            self.send(self.part, self.swap.at[mine], device, spot, 1)
-
-    def gather(self):
+        self.fold()
+        swap, *sems = self.scratch[:3]
+        self.scratch = self.scratch[3:]
+        mine = member(self.last)
+        swap[mine] = self.now[...]
+        for spot, (_, device) in enumerate(peers(self.last)):
+            self.send(self.now, swap.at[mine], device, spot, sems)
+        self.swap = swap
+
+    def settle(self):
         self.wait()
         total = self.swap[0]
-        for index in range(1, group_size(self.second)):
+        for index in range(1, group_size(self.last)):
             total = total + self.swap[index]
-        self.out[self.home] = total
-        for spot, (_, device) in enumerate(peers(self.first)):
-            self.send(self.out.at[self.home], self.out.at[self.home], device, spot, 2)
-
-
-def reducer_scratch(first, second, rows, width):
-    one, two = group_size(first), group_size(second)
-    piece = rows // one
+        start, piece = self.homes[-1]
+        self.out[pl.ds(pl.multiple_of(start, 8), piece)] = total
+        self.gather(self.groups[-1])
+
+    def gather(self, group):
+        self.wait()
+        start, piece = self.homes.pop()
+        sems = self.scratch[:2]
+        self.scratch = self.scratch[2:]
+        home = self.out.at[pl.ds(pl.multiple_of(start, 8), piece)]
+        for spot, (_, device) in enumerate(peers(group)):
+            self.send(home, home, device, spot, sems)
+
+
+def reducer_scratch(groups, last, rows, width):
     dma = pltpu.SemaphoreType.DMA
-    return [
-        pltpu.VMEM((one - 1, piece, width), jnp.float32),
-        pltpu.VMEM((two, piece, width), jnp.float32),
-        pltpu.VMEM((piece, width), jnp.float32),
-        dma((one - 1,)),
-        dma((one - 1,)),
-        dma((two - 1,)),
-        dma((two - 1,)),
-        dma((one - 1,)),
-        dma((one - 1,)),
-    ]
+    found = []
+    for group in groups:
+        count = group_size(group)
+        rows = rows // count
+        found += [pltpu.VMEM((max(count - 1, 1), rows, width), jnp.float32)]
+        found += [pltpu.VMEM((rows, width), jnp.float32)]
+        found += [dma((max(count - 1, 1),))] * 2
+    count = group_size(last)
+    found += [pltpu.VMEM((count, rows, width), jnp.float32)] + [dma((max(count - 1, 1),))] * 2
+    for group in groups[::-1]:
+        found += [dma((max(group_size(group) - 1, 1),))] * 2
+    return found
 
 
 def tiles(rows, size):
@@ -206,73 +241,38 @@
     return {axis: lax.rem(lax.axis_index(axis) + step, count)}
 
 
-def block_kernel(
-    sizes,
-    edge_scale,
-    node_scale,
-    node,
-    ghost,
-    edge,
-    snd,
-    rcv,
-    faces,
-    ncot,
-    ecot,
-    we1,
-    weh,
-    be,
-    ge,
-    se,
-    wn1,
-    wnh,
-    bn,
-    gn,
-    node_o,
-    edge_o,
-    nred_o,
-    ared_o,
-    bred_o,
-    node_id,
-    snd_col,
-    rcv_col,
-    table,
-    z1_s,
-    z2_s,
-    r1_s,
-    slope1_s,
-    slope2_s,
-    normed_s,
-    inv_s,
-    npack,
-    apack,
-    bpack,
-    edge_s,
-    ecot_s,
-    ghost_s,
-    halo,
-    loads,
-    hsend,
-    hland,
-    *scratch,
-):
+INPUTS = 17
+
+
+def block_kernel(sizes, edge_scale, node_scale, counts, *refs):
+    refs = list(refs)
+    take = lambda count: [refs.pop(0) for _ in range(count)]
+    sources = take(INPUTS)
+    node_o, edge_o, nred_o, bred_o, ared_o, be_o, ge_o, se_o, bn_o, gn_o = take(10)
+    held = take(INPUTS)
+    node, ghost, edge, snd, rcv, faces, ncot, ecot, we1, weh, be, ge, se, wn1, wnh, bn, gn = held
+    node_id, lane_id, snd_col, rcv_col, table, z1_s, z2_s, r1_s, slope1_s, slope2_s, normed_s, inv_s = take(12)
+    npack, bpack, apack, ghost_s, halo, loads, hsend, hland = take(8)
+    scratch = [take(count) for count in counts]
     nodes, width = node.shape
     edges = edge.shape[0]
     ghosts = ghost.shape[0]
     slots = ghosts // 6
     total = nodes + ghosts
     bf16, f32 = jnp.bfloat16, jnp.float32
-    near, far = stage_groups(sizes)
-    third = len(scratch) // 3
-    node_red = Reducer(near, far, npack, nred_o, scratch[:third])
-    a_red = Reducer(near, far, apack, ared_o, scratch[third : 2 * third])
-    b_red = Reducer(far, near, bpack, bred_o, scratch[2 * third :])
+    core, chips, near, far = stage_groups(sizes)
+    node_red = Reducer([core, chips], far, npack, nred_o, scratch[0])
+    b_red = Reducer([near], far, bpack, bred_o, scratch[1])
+    a_red = Reducer([near], far, apack, ared_o, scratch[2])
 
     loaded = [
-        pltpu.make_async_copy(edge, edge_s, loads.at[0]),
-        pltpu.make_async_copy(ecot, ecot_s, loads.at[1]),
+        pltpu.make_async_copy(source, target, loads.at[index])
+        for index, (source, target) in enumerate(zip(sources, held))
     ]
-    for copy in loaded:
-        copy.start()
+    order = [4, 3, 8, 0, 1, 2, 9, 10, 11, 12, 6, 13, 14, 15, 16, 7, 5]
+    for index in order:
+        loaded[index].start()
+    arrive = lambda *which: [loaded[index].wait() for index in which]
     barrier = pltpu.get_barrier_semaphore()
     greeted = [face_target(sizes, face) for face in range(6)]
     for group in (near, far):
@@ -280,16 +280,18 @@
     for device in greeted:
         pl.semaphore_signal(barrier, inc=1, device_id=device, device_id_type=MESH)
 
-    lane = lax.broadcasted_iota(jnp.int32, (LANES, LANES), 1).astype(jnp.int16)
+    lane = lax.broadcasted_iota(jnp.int32, (16, LANES), 1)
     sub = lax.broadcasted_iota(jnp.int32, (LANES, LANES), 0)
     one = jnp.ones((LANES, LANES), bf16)
     zero = jnp.zeros((LANES, LANES), bf16)
     for part in range(total // LANES):
         node_id[part] = (sub + part * LANES).astype(jnp.int16)
+        lane_id[part] = (lane + part * LANES).astype(jnp.int16)
 
     def column(row):
         return jnp.transpose(jnp.broadcast_to(row, (LANES, LANES)))
 
+    arrive(4, 3, 8, 0, 1, 2, 9, 10, 11, 12)
     for block in range(edges // LANES):
         at = slice(block * LANES, (block + 1) * LANES)
         snd_col[block] = column(snd[:, at]).astype(jnp.int16)
@@ -309,7 +311,7 @@
         ids = columns[block]
         return jnp.concatenate(
             [
-                jnp.where(ids == lane + jnp.int16(part * LANES), one, zero)
+                jnp.where(ids == jnp.concatenate([lane_id[part]] * (LANES // 16), 0), one, zero)
                 for part in range(first // LANES, (first + count) // LANES)
             ],
             1,
@@ -336,11 +338,10 @@
     put_blocks(table, total, matmul_nt(w1[2], node[...]).astype(bf16))
     spots = (total + nodes) // LANES
 
-    loaded[0].wait()
     agg = None
     for start, size in tiles(edges, FORWARD_TILE):
         at = pl.ds(start, size)
-        rights = [jnp.transpose(edge_s[at])]
+        rights = [jnp.transpose(edge[at])]
         rights += node_hots(snd, start, size, total) + node_hots(rcv, start, size, nodes)
         first = chain([w1[0]] + [table[spot] for spot in range(spots)], rights)
         act, slope = silu_parts(first + wide(bias[0], size))
@@ -360,6 +361,7 @@
         term = chain(lefts, rights)
         agg = term if agg is None else agg + term
 
+    arrive(6, 13, 14, 15, 16)
     agg = agg.astype(bf16)
     n1a, n1b = half_t(wn1[:width]), half_t(wn1[width:])
     n2, n3 = half_t(wnh[0]), jnp.transpose(wnh[1])
@@ -383,7 +385,7 @@
     node_terms += [matmul_nt(z1, r2), matmul_nt(z2, r3)]
     for index, term in enumerate(node_terms):
         npack[index * width : (index + 1) * width] = term * node_scale
-    for pack, used in ((npack, 4 * width), (apack, 4 * width), (bpack, width)):
+    for pack, used in ((npack, 4 * width), (apack, 2 * width), (bpack, 3 * width)):
         if pack.shape[0] > used:
             pack[used:] = jnp.zeros((pack.shape[0] - used, width), f32)
 
@@ -392,19 +394,19 @@
 
     node_sums = (lane_fold(g1), lane_fold(g2), lane_fold(g3), gain_sum)
     for index, value in enumerate(node_sums):
-        bpack[width + 5 + index : width + 6 + index] = row_of(value) * node_scale
+        bpack[3 * width + 5 + index : 3 * width + 6 + index] = row_of(value) * node_scale
 
     pl.semaphore_wait(barrier, len(greeted))
-    node_red.scatter()
-
-    loaded[1].wait()
+    node_red.advance()
+
+    arrive(7)
     small = [None] * 5
     grads = [None] * 3
     more = lambda old, new: new if old is None else old + new
     lefts = [agg_grad[:, spot : spot + LANES] for spot in range(0, nodes, LANES)]
     for start, size in tiles(edges, BACKWARD_TILE):
         at = pl.ds(start, size)
-        up = jnp.transpose(ecot_s[at]).astype(f32)
+        up = jnp.transpose(ecot[at]).astype(f32)
         up = up + chain(lefts, node_hots(rcv, start, size, nodes))
         normed = blocks_of(normed_s, start, size)
         g3 = norm_back(up * wide(gain, size), normed, blocks_of(inv_s, start, size))
@@ -414,11 +416,20 @@
         g1 = matmul(back2, r2) * blocks_of(slope1_s, start, size)
         r1 = g1.astype(bf16)
         put_blocks(r1_s, start, r1)
-        grads[0] = more(grads[0], matmul(r1, edge_s[at]))
+        grads[0] = more(grads[0], matmul(r1, edge[at]))
         grads[1] = more(grads[1], matmul_nt(blocks_of(z1_s, start, size), r2))
         grads[2] = more(grads[2], matmul_nt(blocks_of(z2_s, start, size), r3))
         for index, term in enumerate((g1, g2, g3, up * normed, up)):
             small[index] = more(small[index], lane_fold(term))
+        if start == 0:
+            node_red.advance()
+
+    for index, term in enumerate((jnp.transpose(grads[0]), grads[1], grads[2])):
+        bpack[index * width : (index + 1) * width] = term * edge_scale
+    for index, value in enumerate(small):
+        bpack[3 * width + index : 3 * width + 1 + index] = row_of(value) * edge_scale
+    b_red.advance()
+    node_red.advance()
 
     lefts = [r1_s[block] for block in range(edges // LANES)]
     by_sender = []
@@ -433,15 +444,9 @@
     by_receiver = jnp.concatenate(by_receiver, 1)
     middle = matmul(by_sender[:, :nodes], node[...]) + matmul(by_sender[:, nodes:], ghost[...])
     last = matmul(by_receiver, node[...])
-    turned = [jnp.transpose(term) for term in (grads[0], middle, last)]
-    for index, term in enumerate(turned + [grads[1]]):
-        apack[index * width : (index + 1) * width] = term * edge_scale
-    bpack[:width] = grads[2] * edge_scale
-    for index, value in enumerate(small):
-        bpack[width + index : width + 1 + index] = row_of(value) * edge_scale
-    a_red.scatter()
-    b_red.scatter()
-    node_red.exchange()
+    apack[:width] = jnp.transpose(middle) * edge_scale
+    apack[width : 2 * width] = jnp.transpose(last) * edge_scale
+    a_red.advance()
 
     full = matmul(we1[width : 2 * width], by_sender)
     ghost_s[...] = jnp.transpose(full[:, nodes:])
@@ -464,51 +469,66 @@
     def edge_out(first, last):
         for block in range(first, last):
             at = pl.ds(block * LANES, LANES)
-            grad = ecot_s[at].astype(f32) + matmul_nt(jnp.transpose(r1_s[block]), we1[:width])
+            grad = ecot[at].astype(f32) + matmul_nt(jnp.transpose(r1_s[block]), we1[:width])
             edge_o[at] = grad.astype(bf16)
 
     middle_block = edges // LANES // 2
     edge_out(0, middle_block)
-    a_red.exchange()
-    b_red.exchange()
-    node_red.gather()
+    b_red.advance()
+    node_red.advance()
     edge_out(middle_block, edges // LANES)
+    a_red.advance()
+    b_red.advance()
+    node_red.advance()
     for copy in halos:
         copy.wait()
+    arrive(5)
     spot = lax.broadcasted_iota(jnp.int32, (nodes, slots), 0)
     local = node_o[...]
     for face in range(6):
         values = halo[face * slots : (face + 1) * slots].astype(bf16)
         local = local + matmul(one_hot(spot == faces[face]), values)
     node_o[...] = local
-    a_red.gather()
-    b_red.gather()
-    node_red.wait()
-    a_red.wait()
-    b_red.wait()
-
-
-def finish_kernel(
-    node, edge, nred, ared, bred, node_o, edge_o, we1_o, weh_o, be_o, ge_o, se_o, wn1_o, wnh_o, bn_o, gn_o
-):
+    a_red.advance()
+    b_red.advance()
+    for start, target in ((0, be_o), (3, ge_o), (4, se_o), (5, bn_o), (8, gn_o)):
+        start = 3 * width + start
+        target[...] = bred_o[start : start + target.shape[0]]
+    node_red.advance()
+    a_red.advance()
+
+
+def finish_kernel(node, edge, nred, bred, ared, be, ge, se, bn, gn, *refs):
+    node_o, edge_o, we1_o, weh_o, be_o, ge_o, se_o, wn1_o, wnh_o, bn_o, gn_o, sems = refs
     width = node.shape[1]
-    node_o[...] = node[...]
-    edge_o[...] = edge[...]
-    we1_o[...] = ared[: 3 * width]
-    weh_o[0] = ared[3 * width : 4 * width]
-    weh_o[1] = bred[:width]
-    wn1_o[...] = nred[: 2 * width]
-    wnh_o[0] = nred[2 * width : 3 * width]
-    wnh_o[1] = nred[3 * width : 4 * width]
-    be_o[...] = bred[width : width + 3]
-    ge_o[...] = bred[width + 3 : width + 4]
-    se_o[...] = bred[width + 4 : width + 5]
-    bn_o[...] = bred[width + 5 : width + 8]
-    gn_o[...] = bred[width + 8 : width + 9]
+    pairs = [
+        (edge, edge_o),
+        (node, node_o),
+        (bred.at[:width], we1_o.at[:width]),
+        (ared.at[: 2 * width], we1_o.at[width:]),
+        (bred.at[width : 2 * width], weh_o.at[0]),
+        (bred.at[2 * width : 3 * width], weh_o.at[1]),
+        (nred.at[: 2 * width], wn1_o),
+        (nred.at[2 * width : 3 * width], wnh_o.at[0]),
+        (nred.at[3 * width : 4 * width], wnh_o.at[1]),
+        (be, be_o),
+        (ge, ge_o),
+        (se, se_o),
+        (bn, bn_o),
+        (gn, gn_o),
+    ]
+    copies = [
+        pltpu.make_async_copy(source, target, sems.at[index])
+        for index, (source, target) in enumerate(pairs)
+    ]
+    for copy in copies:
+        copy.start()
+    for copy in copies:
+        copy.wait()
 
 
 VMEM = pl.BlockSpec(memory_space=pltpu.VMEM)
-HBM = pl.BlockSpec(memory_space=pl.ANY)
+HBM = pl.BlockSpec(memory_space=pltpu.HBM)
 
 
 def on_device(
@@ -541,58 +561,25 @@
     edge_scale = float(edges * devices) ** (-0.5)
     node_scale = float(nodes * devices) ** (-0.5)
 
-    def padded(rows, group):
-        unit = 8 * group_size(group)
+    def padded(rows, *groups):
+        unit = 8
+        for group in groups:
+            unit *= group_size(group)
         return -(-rows // unit) * unit
 
     def shape(*dims, dtype=f32):
         return jax.ShapeDtypeStruct(dims, dtype)
 
-    near, far = stage_groups(sizes)
-    four, two = padded(4 * width, near), padded(width + 9, far)
-    reducers = reducer_scratch(near, far, four, width)
-    reducers += reducer_scratch(near, far, four, width)
-    reducers += reducer_scratch(far, near, two, width)
-    passed = pl.pallas_call(
-        functools.partial(block_kernel, sizes, edge_scale, node_scale),
-        out_shape=(
-            shape(nodes, width),
-            shape(edges, width, dtype=bf16),
-            shape(four, width),
-            shape(four, width),
-            shape(two, width),
-        ),
-        in_specs=[VMEM] * 2 + [HBM] + [VMEM] * 4 + [HBM] + [VMEM] * 9,
-        out_specs=(VMEM,) * 5,
-        scratch_shapes=[
-            pltpu.VMEM((total // LANES, LANES, LANES), jnp.int16),
-            pltpu.VMEM((edges // LANES, LANES, LANES), jnp.int16),
-            pltpu.VMEM((edges // LANES, LANES, LANES), jnp.int16),
-            pltpu.VMEM(((total + nodes) // LANES, LANES, LANES), bf16),
-            pltpu.VMEM((edges // LANES, LANES, LANES), bf16),
-            pltpu.VMEM((edges // LANES, LANES, LANES), bf16),
-            pltpu.VMEM((edges // LANES, LANES, LANES), bf16),
-            pltpu.VMEM((edges // LANES, LANES, LANES), f32),
-            pltpu.VMEM((edges // LANES, LANES, LANES), f32),
-            pltpu.VMEM((edges // LANES, LANES, LANES), f32),
-            pltpu.VMEM((edges // LANES, 1, LANES), f32),
-            pltpu.VMEM((four, width), f32),
-            pltpu.VMEM((four, width), f32),
-            pltpu.VMEM((two, width), f32),
-            pltpu.VMEM((edges, width), bf16),
-            pltpu.VMEM((edges, width), bf16),
-            pltpu.VMEM((ghosts, width), f32),
-            pltpu.VMEM((ghosts, width), f32),
-            pltpu.SemaphoreType.DMA((2,)),
-            pltpu.SemaphoreType.DMA((6,)),
-            pltpu.SemaphoreType.DMA((6,)),
-        ]
-        + reducers,
-        compiler_params=pltpu.CompilerParams(
-            collective_id=0, has_side_effects=True, vmem_limit_bytes=60 * 1024 * 1024
-        ),
-        name="block_pass",
-    )(
+    core, chips, near, far = stage_groups(sizes)
+    nrows = padded(4 * width, core, chips)
+    brows = padded(3 * width + 9, near)
+    arows = padded(2 * width, near)
+    reducers = [
+        reducer_scratch([core, chips], far, nrows, width),
+        reducer_scratch([near], far, brows, width),
+        reducer_scratch([near], far, arows, width),
+    ]
+    operands = (
         node_latent.reshape(nodes, width),
         ghost_latent.reshape(ghosts, width),
         edge_latent.reshape(edges, width),
@@ -611,6 +598,53 @@
         b_node,
         gain_node.reshape(1, width),
     )
+    operands = [pltpu.with_memory_space_constraint(operand, pltpu.HBM) for operand in operands]
+    counts = [len(found) for found in reducers]
+    passed = pl.pallas_call(
+        functools.partial(block_kernel, sizes, edge_scale, node_scale, counts),
+        out_shape=(
+            shape(nodes, width),
+            shape(edges, width, dtype=bf16),
+            shape(nrows, width),
+            shape(brows, width),
+            shape(arows, width),
+            shape(3, width),
+            shape(1, width),
+            shape(1, width),
+            shape(3, width),
+            shape(1, width),
+        ),
+        in_specs=[HBM] * INPUTS,
+        out_specs=(VMEM,) * 10,
+        scratch_shapes=[pltpu.VMEM(operand.shape, operand.dtype) for operand in operands]
+        + [
+            pltpu.VMEM((total // LANES, LANES, LANES), jnp.int16),
+            pltpu.VMEM((total // LANES, 16, LANES), jnp.int16),
+            pltpu.VMEM((edges // LANES, LANES, LANES), jnp.int16),
+            pltpu.VMEM((edges // LANES, LANES, LANES), jnp.int16),
+            pltpu.VMEM(((total + nodes) // LANES, LANES, LANES), bf16),
+            pltpu.VMEM((edges // LANES, LANES, LANES), bf16),
+            pltpu.VMEM((edges // LANES, LANES, LANES), bf16),
+            pltpu.VMEM((edges // LANES, LANES, LANES), bf16),
+            pltpu.VMEM((edges // LANES, LANES, LANES), f32),
+            pltpu.VMEM((edges // LANES, LANES, LANES), f32),
+            pltpu.VMEM((edges // LANES, LANES, LANES), f32),
+            pltpu.VMEM((edges // LANES, 1, LANES), f32),
+            pltpu.VMEM((nrows, width), f32),
+            pltpu.VMEM((brows, width), f32),
+            pltpu.VMEM((arows, width), f32),
+            pltpu.VMEM((ghosts, width), f32),
+            pltpu.VMEM((ghosts, width), f32),
+            pltpu.SemaphoreType.DMA((INPUTS,)),
+            pltpu.SemaphoreType.DMA((6,)),
+            pltpu.SemaphoreType.DMA((6,)),
+        ]
+        + sum(reducers, []),
+        compiler_params=pltpu.CompilerParams(
+            collective_id=0, has_side_effects=True, vmem_limit_bytes=32 * 1024 * 1024
+        ),
+        name="block_pass",
+    )(*operands)
 
     outs = pl.pallas_call(
         finish_kernel,
@@ -627,8 +661,10 @@
             shape(3, width),
             shape(1, width),
         ),
-        in_specs=[VMEM] * 5,
-        out_specs=(VMEM,) * 11,
+        in_specs=[VMEM] * 10,
+        out_specs=(HBM,) * 11,
+        scratch_shapes=[pltpu.SemaphoreType.DMA((14,))],
+        compiler_params=pltpu.CompilerParams(vmem_limit_bytes=4 * 1024 * 1024),
         name="finish",
     )(*passed)
     node_grad, edge_grad, we1, weh, be, ge, se, wn1, wnh, bn, gn = outs

time: 38.4 us -> 32.2 us (0.84)
  Pallas kernels: 37.6 us -> 31.3 us
    pallas_call x1, Pallas kernels: 35.1 us -> 30.1 us  [on_device(): pl.pallas_call(functools.partial(block_kernel, sizes, edge_scale, node_sc...]
    pallas_call x1, Pallas kernels: 2.54 us -> 1.27 us  [on_device(): pl.pallas_call(finish_kernel, out_shape=(shape(nodes, width), shape(edges...]
where the time goes in v2:
time: 32.2 us; the launch traced here: 32 us
  Pallas kernels  31.3 us (97%)
  between operations  0.66 us (2%)
    pallas_call x1, Pallas kernels, on_device(): pl.pallas_call(functools.partial(block_kernel, sizes, edge_scale, node_sc...  30.1 us
    pallas_call x1, Pallas kernels, on_device(): pl.pallas_call(finish_kernel, out_shape=(shape(nodes, width), shape(edges...  1.27 us

profile of v2, /device:TPU:0, one launch (start us, length us, event | category | flops | bytes accessed | tf_op | source)
XLA Modules:
  0.0 32.0 jit_solution(15040757903744125458)
XLA Ops:
  0.7 30.1 %block_pass.1 = (f32[512,128]{1,0:T(8,128)S(1)}, bf16[2816,128]{1,0:T(8,128)(2,1)S(1)}, f32[512,128]{1,0:T(8,128)S(1)}, f32[448,128]{1,0:T(8,128)S(1)}, f32[256,...) custom-call(bf16[512,128]{1,0:T(8,128)(2,1)} %bitcast.18, ...), custom_call_target="tpu_custom_call" | custom-call | tf_op jit(solution)/shard_map/block_pass/pallas_call | solution.py:603
  30.7 1.3 %finish.1 = (f32[512,128]{1,0:T(8,128)}, bf16[2816,128]{1,0:T(8,128)(2,1)}, f32[384,128]{1,0:T(8,128)}, f32[2,128,128]{2,1,0:T(8,128)}, f32[3,128]{1,0:T(4,128)}...) custom-call(f32[512,128]{1,0:T(8,128)S(1)} %get-tuple-element.32.nod, ...), custom_call_target="tpu_custom_call" | custom-call | tf_op jit(solution)/shard_map/finish/pallas_call | solution.py:649

commit v3 on v2

--- a/solution.py
+++ b/solution.py
@@ -9,8 +9,11 @@
 
 EPSILON = 1e-05
 LANES = 128
-FORWARD_TILE = 1408
-BACKWARD_TILE = 1408
+KINDS = {"N": "near", "B": "near", "A": "near"}
+PLAN = {"node": "N", "edge": "B", "scatter": "AN", "out1": "B", "out2": "A", "out3": "N", "late": "BAB", "end": "NA"}
+HALO = -1
+FORWARD_TILE = 768
+BACKWARD_TILE = 512
 MESH = pl.DeviceIdType.MESH
 AXES = ("gx", "gy", "gz")
 
@@ -85,9 +88,26 @@
     pair = 2 if sizes["gz"] % 2 == 0 else 1
     core = [("gz", pair, 1)]
     chips = [("gx", sizes["gx"], 1), ("gz", sizes["gz"] // pair, pair)]
-    near = [("gx", sizes["gx"], 1), ("gz", sizes["gz"], 1)]
+    near = core + chips
     far = [("gy", sizes["gy"], 1)]
     return core, chips, near, far
+
+
+def set_groups(sizes):
+    core, chips, near, far = stage_groups(sizes)
+    count = sizes["gy"]
+    twice = [far]
+    if count % 2 == 0 and count > 2:
+        twice = [[("gy", 2, 1)], [("gy", count // 2, 2)]]
+    kinds = {
+        "near": ([near], [far], [near]),
+        "near2": ([near], twice, [near]),
+        "core": ([core, chips], [far], [chips, core]),
+        "core2": ([core, chips], twice, [chips, core]),
+        "mix": ([near], [far], [chips, core]),
+        "mix2": ([near], twice, [chips, core]),
+    }
+    return {name: kinds[kind] for name, kind in KINDS.items()}
 
 
 def group_size(group):
@@ -129,15 +149,16 @@
 
 
 class Reducer:
-    def __init__(self, groups, last, source, out, scratch):
-        self.groups, self.last, self.source, self.out = groups, last, source, out
+    def __init__(self, down, lasts, up, source, out, scratch):
+        self.out, self.swap = out, None
         self.scratch = list(scratch)
         self.now, self.spot, self.rows = source, 0, source.shape[0]
-        self.homes = []
+        self.arrived = None
         self.pending = []
-        self.steps = [functools.partial(self.scatter, group) for group in groups]
-        self.steps += [self.exchange, self.settle]
-        self.steps += [functools.partial(self.gather, group) for group in groups[-2::-1]]
+        self.steps = [functools.partial(self.scatter, group) for group in down]
+        self.steps += [functools.partial(self.exchange, group) for group in lasts]
+        self.steps += [functools.partial(self.settle, up[0])]
+        self.steps += [functools.partial(self.gather, group) for group in up[1:]]
         self.steps += [self.wait]
 
     def advance(self):
@@ -161,7 +182,7 @@
         self.pending = []
 
     def fold(self):
-        if not self.homes:
+        if self.arrived is None:
             return
         self.wait()
         landing, part, own = self.arrived
@@ -182,56 +203,76 @@
         self.count = group_size(group) - 1
         mine = member(group) * piece
         self.spot = self.spot + mine
-        self.homes.append((self.spot, piece))
         self.arrived = landing, part, self.now.at[pl.ds(pl.multiple_of(mine, 8), piece)]
 
-    def exchange(self):
-        self.fold()
+    def swapped(self):
+        self.wait()
+        total = self.swap[0]
+        for index in range(1, self.count):
+            total = total + self.swap[index]
+        return total
+
+    def exchange(self, group):
+        if self.swap is None:
+            self.fold()
+        else:
+            total = self.swapped()
+            self.now = self.scratch.pop(0)
+            self.now[...] = total
         swap, *sems = self.scratch[:3]
         self.scratch = self.scratch[3:]
-        mine = member(self.last)
+        mine = member(group)
         swap[mine] = self.now[...]
-        for spot, (_, device) in enumerate(peers(self.last)):
+        for spot, (_, device) in enumerate(peers(group)):
             self.send(self.now, swap.at[mine], device, spot, sems)
-        self.swap = swap
-
-    def settle(self):
-        self.wait()
-        total = self.swap[0]
-        for index in range(1, group_size(self.last)):
-            total = total + self.swap[index]
-        start, piece = self.homes[-1]
-        self.out[pl.ds(pl.multiple_of(start, 8), piece)] = total
-        self.gather(self.groups[-1])
+        self.swap, self.count = swap, group_size(group)
+
+    def settle(self, group):
+        total = self.swapped()
+        self.piece = self.now.shape[0]
+        self.out[pl.ds(pl.multiple_of(self.spot, 8), self.piece)] = total
+        self.gather(group)
 
     def gather(self, group):
         self.wait()
-        start, piece = self.homes.pop()
         sems = self.scratch[:2]
         self.scratch = self.scratch[2:]
-        home = self.out.at[pl.ds(pl.multiple_of(start, 8), piece)]
+        home = self.out.at[pl.ds(pl.multiple_of(self.spot, 8), self.piece)]
         for spot, (_, device) in enumerate(peers(group)):
             self.send(home, home, device, spot, sems)
-
-
-def reducer_scratch(groups, last, rows, width):
+        self.spot = self.spot - member(group) * self.piece
+        self.piece = self.piece * group_size(group)
+
+
+def reducer_scratch(down, lasts, up, rows, width):
     dma = pltpu.SemaphoreType.DMA
     found = []
-    for group in groups:
+    for group in down:
         count = group_size(group)
         rows = rows // count
         found += [pltpu.VMEM((max(count - 1, 1), rows, width), jnp.float32)]
         found += [pltpu.VMEM((rows, width), jnp.float32)]
         found += [dma((max(count - 1, 1),))] * 2
-    count = group_size(last)
-    found += [pltpu.VMEM((count, rows, width), jnp.float32)] + [dma((max(count - 1, 1),))] * 2
-    for group in groups[::-1]:
+    for index, group in enumerate(lasts):
+        count = group_size(group)
+        if index:
+            found += [pltpu.VMEM((rows, width), jnp.float32)]
+        found += [pltpu.VMEM((count, rows, width), jnp.float32)] + [dma((max(count - 1, 1),))] * 2
+    for group in up:
         found += [dma((max(group_size(group) - 1, 1),))] * 2
     return found
 
 
 def tiles(rows, size):
     return [(start, min(size, rows - start)) for start in range(0, rows, size)]
+
+
+def stagger(stages, cuts):
+    waiting, running = [stages(*cut) for cut in cuts], []
+    while waiting or running:
+        if waiting:
+            running.insert(0, waiting.pop(0))
+        running = [tile for tile in running if next(tile, "done") != "done"]
 
 
 def face_target(sizes, face):
@@ -251,7 +292,7 @@
     node_o, edge_o, nred_o, bred_o, ared_o, be_o, ge_o, se_o, bn_o, gn_o = take(10)
     held = take(INPUTS)
     node, ghost, edge, snd, rcv, faces, ncot, ecot, we1, weh, be, ge, se, wn1, wnh, bn, gn = held
-    node_id, lane_id, snd_col, rcv_col, table, z1_s, z2_s, r1_s, slope1_s, slope2_s, normed_s, inv_s = take(12)
+    node_id, snd_col, rcv_col, table, z1_s, z2_s, r1_s, slope1_s, slope2_s, normed_s, inv_s = take(11)
     npack, bpack, apack, ghost_s, halo, loads, hsend, hland = take(8)
     scratch = [take(count) for count in counts]
     nodes, width = node.shape
@@ -261,9 +302,16 @@
     total = nodes + ghosts
     bf16, f32 = jnp.bfloat16, jnp.float32
     core, chips, near, far = stage_groups(sizes)
-    node_red = Reducer([core, chips], far, npack, nred_o, scratch[0])
-    b_red = Reducer([near], far, bpack, bred_o, scratch[1])
-    a_red = Reducer([near], far, apack, ared_o, scratch[2])
+    groups = set_groups(sizes)
+    node_red = Reducer(*groups["N"], npack, nred_o, scratch[0])
+    b_red = Reducer(*groups["B"], bpack, bred_o, scratch[1])
+    a_red = Reducer(*groups["A"], apack, ared_o, scratch[2])
+
+    chains = {"N": node_red, "B": b_red, "A": a_red}
+
+    def reach(point):
+        for name in PLAN.get(point, ""):
+            chains[name].advance()
 
     loaded = [
         pltpu.make_async_copy(source, target, loads.at[index])
@@ -280,13 +328,11 @@
     for device in greeted:
         pl.semaphore_signal(barrier, inc=1, device_id=device, device_id_type=MESH)
 
-    lane = lax.broadcasted_iota(jnp.int32, (16, LANES), 1)
     sub = lax.broadcasted_iota(jnp.int32, (LANES, LANES), 0)
     one = jnp.ones((LANES, LANES), bf16)
     zero = jnp.zeros((LANES, LANES), bf16)
     for part in range(total // LANES):
         node_id[part] = (sub + part * LANES).astype(jnp.int16)
-        lane_id[part] = (lane + part * LANES).astype(jnp.int16)
 
     def column(row):
         return jnp.transpose(jnp.broadcast_to(row, (LANES, LANES)))
@@ -307,15 +353,21 @@
             for part in range(count // LANES)
         ]
 
+    def lanes_of(part):
+        spot = lax.broadcasted_iota(jnp.int32, (LANES, LANES), 1) + part * LANES
+        return spot.astype(jnp.int16)
+
     def edge_hots(columns, block, first, count):
         ids = columns[block]
         return jnp.concatenate(
             [
-                jnp.where(ids == jnp.concatenate([lane_id[part]] * (LANES // 16), 0), one, zero)
+                jnp.where(lanes_of(part) == ids, one, zero)
                 for part in range(first // LANES, (first + count) // LANES)
             ],
             1,
         )
+
+    more = lambda old, new: new if old is None else old + new
 
     def blocks_of(ref, start, size):
         spots = range(start // LANES, (start + size) // LANES)
@@ -333,36 +385,42 @@
     bias = [column(0.5 * be[0:1]), column(0.5 * be[1:2]), column(be[2:3])]
     gain, shift = column(ge[...]), column(se[...])
 
-    put_blocks(table, 0, matmul_nt(w1[1], node[...]).astype(bf16))
-    put_blocks(table, nodes, matmul_nt(w1[1], ghost[...]).astype(bf16))
+    put_blocks(table, 0, (matmul_nt(w1[1], node[...]) + wide(bias[0], nodes)).astype(bf16))
+    put_blocks(table, nodes, (matmul_nt(w1[1], ghost[...]) + wide(bias[0], ghosts)).astype(bf16))
     put_blocks(table, total, matmul_nt(w1[2], node[...]).astype(bf16))
     spots = (total + nodes) // LANES
 
-    agg = None
-    for start, size in tiles(edges, FORWARD_TILE):
-        at = pl.ds(start, size)
-        rights = [jnp.transpose(edge[at])]
+    agg = [None]
+
+    def forward(start, size):
+        rights = [jnp.transpose(edge[pl.ds(start, size)])]
         rights += node_hots(snd, start, size, total) + node_hots(rcv, start, size, nodes)
         first = chain([w1[0]] + [table[spot] for spot in range(spots)], rights)
-        act, slope = silu_parts(first + wide(bias[0], size))
+        yield
+        act, slope = silu_parts(first)
         z1 = act.astype(bf16)
         put_blocks(z1_s, start, z1)
         put_blocks(slope1_s, start, slope)
-        act, slope = silu_parts(matmul(w2, z1) + wide(bias[1], size))
+        second = matmul(w2, z1)
+        yield
+        act, slope = silu_parts(second + wide(bias[1], size))
         z2 = act.astype(bf16)
         put_blocks(z2_s, start, z2)
         put_blocks(slope2_s, start, slope)
-        normed, inv = norm_parts(matmul(w3, z2) + wide(bias[2], size))
+        third = matmul(w3, z2)
+        yield
+        normed, inv = norm_parts(third + wide(bias[2], size))
         put_blocks(normed_s, start, normed)
         put_blocks(inv_s, start, inv)
         new = (normed * wide(gain, size) + wide(shift, size)).astype(bf16)
         lefts = [new[:, spot : spot + LANES] for spot in range(0, size, LANES)]
         rights = [edge_hots(rcv_col, (start + spot) // LANES, 0, nodes) for spot in range(0, size, LANES)]
-        term = chain(lefts, rights)
-        agg = term if agg is None else agg + term
+        agg[0] = more(agg[0], chain(lefts, rights))
+
+    stagger(forward, tiles(edges, FORWARD_TILE))
 
     arrive(6, 13, 14, 15, 16)
-    agg = agg.astype(bf16)
+    agg = agg[0].astype(bf16)
     n1a, n1b = half_t(wn1[:width]), half_t(wn1[width:])
     n2, n3 = half_t(wnh[0]), jnp.transpose(wnh[1])
     first = matmul_nt(n1a, node[...]) + matmul(n1b, agg)
@@ -397,45 +455,52 @@
         bpack[3 * width + 5 + index : 3 * width + 6 + index] = row_of(value) * node_scale
 
     pl.semaphore_wait(barrier, len(greeted))
-    node_red.advance()
+    reach("node")
 
     arrive(7)
     small = [None] * 5
     grads = [None] * 3
-    more = lambda old, new: new if old is None else old + new
     lefts = [agg_grad[:, spot : spot + LANES] for spot in range(0, nodes, LANES)]
-    for start, size in tiles(edges, BACKWARD_TILE):
+
+    def backward(start, size):
         at = pl.ds(start, size)
         up = jnp.transpose(ecot[at]).astype(f32)
         up = up + chain(lefts, node_hots(rcv, start, size, nodes))
+        yield
         normed = blocks_of(normed_s, start, size)
         g3 = norm_back(up * wide(gain, size), normed, blocks_of(inv_s, start, size))
         r3 = g3.astype(bf16)
-        g2 = matmul(back3, r3) * blocks_of(slope2_s, start, size)
+        for index, term in ((2, g3), (3, up * normed), (4, up)):
+            small[index] = more(small[index], lane_fold(term))
+        second = matmul(back3, r3)
+        grads[2] = more(grads[2], matmul_nt(blocks_of(z2_s, start, size), r3))
+        yield
+        g2 = second * blocks_of(slope2_s, start, size)
         r2 = g2.astype(bf16)
-        g1 = matmul(back2, r2) * blocks_of(slope1_s, start, size)
+        small[1] = more(small[1], lane_fold(g2))
+        first = matmul(back2, r2)
+        grads[1] = more(grads[1], matmul_nt(blocks_of(z1_s, start, size), r2))
+        yield
+        g1 = first * blocks_of(slope1_s, start, size)
         r1 = g1.astype(bf16)
+        small[0] = more(small[0], lane_fold(g1))
         put_blocks(r1_s, start, r1)
         grads[0] = more(grads[0], matmul(r1, edge[at]))
-        grads[1] = more(grads[1], matmul_nt(blocks_of(z1_s, start, size), r2))
-        grads[2] = more(grads[2], matmul_nt(blocks_of(z2_s, start, size), r3))
-        for index, term in enumerate((g1, g2, g3, up * normed, up)):
-            small[index] = more(small[index], lane_fold(term))
-        if start == 0:
-            node_red.advance()
+
+    stagger(backward, tiles(edges, BACKWARD_TILE))
 
     for index, term in enumerate((jnp.transpose(grads[0]), grads[1], grads[2])):
         bpack[index * width : (index + 1) * width] = term * edge_scale
     for index, value in enumerate(small):
         bpack[3 * width + index : 3 * width + 1 + index] = row_of(value) * edge_scale
-    b_red.advance()
-    node_red.advance()
+    reach("edge")
 
     lefts = [r1_s[block] for block in range(edges // LANES)]
     by_sender = []
     for start, size in tiles(total, 2 * LANES):
         rights = [edge_hots(snd_col, block, start, size) for block in range(edges // LANES)]
         by_sender.append(chain(lefts, rights).astype(bf16))
+        reach("part%d" % (start // (2 * LANES)))
     by_receiver = []
     for start, size in tiles(nodes, 2 * LANES):
         rights = [edge_hots(rcv_col, block, start, size) for block in range(edges // LANES)]
@@ -446,40 +511,40 @@
     last = matmul(by_receiver, node[...])
     apack[:width] = jnp.transpose(middle) * edge_scale
     apack[width : 2 * width] = jnp.transpose(last) * edge_scale
-    a_red.advance()
+    reach("scatter")
 
     full = matmul(we1[width : 2 * width], by_sender)
     ghost_s[...] = jnp.transpose(full[:, nodes:])
-    halos = []
-    for face in range(6):
-        rows = pl.ds(face * slots, slots)
-        copy = pltpu.make_async_remote_copy(
-            src_ref=ghost_s.at[rows],
-            dst_ref=halo.at[rows],
-            send_sem=hsend.at[face],
-            recv_sem=hland.at[face],
-            device_id=face_target(sizes, face),
-            device_id_type=MESH,
-        )
-        copy.start()
-        halos.append(copy)
+    def send_halos():
+        halos = []
+        for face in range(6):
+            rows = pl.ds(face * slots, slots)
+            copy = pltpu.make_async_remote_copy(
+                src_ref=ghost_s.at[rows],
+                dst_ref=halo.at[rows],
+                send_sem=hsend.at[face],
+                recv_sem=hland.at[face],
+                device_id=face_target(sizes, face),
+                device_id_type=MESH,
+            )
+            copy.start()
+            halos.append(copy)
+        return halos
+
     node_part = node_part + full[:, :nodes] + matmul(we1[2 * width :], by_receiver)
     node_o[...] = jnp.transpose(node_part)
 
-    def edge_out(first, last):
-        for block in range(first, last):
+    halos = send_halos() if HALO < 0 else []
+    reach("halo")
+    parts = 4
+    for part in range(parts):
+        for block in range(edges // LANES * part // parts, edges // LANES * (part + 1) // parts):
             at = pl.ds(block * LANES, LANES)
             grad = ecot[at].astype(f32) + matmul_nt(jnp.transpose(r1_s[block]), we1[:width])
             edge_o[at] = grad.astype(bf16)
-
-    middle_block = edges // LANES // 2
-    edge_out(0, middle_block)
-    b_red.advance()
-    node_red.advance()
-    edge_out(middle_block, edges // LANES)
-    a_red.advance()
-    b_red.advance()
-    node_red.advance()
+        reach("out%d" % part)
+        if part == HALO:
+            halos = send_halos()
     for copy in halos:
         copy.wait()
     arrive(5)
@@ -489,13 +554,11 @@
         values = halo[face * slots : (face + 1) * slots].astype(bf16)
         local = local + matmul(one_hot(spot == faces[face]), values)
     node_o[...] = local
-    a_red.advance()
-    b_red.advance()
+    reach("late")
     for start, target in ((0, be_o), (3, ge_o), (4, se_o), (5, bn_o), (8, gn_o)):
         start = 3 * width + start
         target[...] = bred_o[start : start + target.shape[0]]
-    node_red.advance()
-    a_red.advance()
+    reach("end")
 
 
 def finish_kernel(node, edge, nred, bred, ared, be, ge, se, bn, gn, *refs):
@@ -570,14 +633,14 @@
     def shape(*dims, dtype=f32):
         return jax.ShapeDtypeStruct(dims, dtype)
 
-    core, chips, near, far = stage_groups(sizes)
-    nrows = padded(4 * width, core, chips)
-    brows = padded(3 * width + 9, near)
-    arows = padded(2 * width, near)
+    groups = set_groups(sizes)
+    nrows = padded(4 * width, *groups["N"][0])
+    brows = padded(3 * width + 9, *groups["B"][0])
+    arows = padded(2 * width, *groups["A"][0])
     reducers = [
-        reducer_scratch([core, chips], far, nrows, width),
-        reducer_scratch([near], far, brows, width),
-        reducer_scratch([near], far, arows, width),
+        reducer_scratch(*groups["N"], nrows, width),
+        reducer_scratch(*groups["B"], brows, width),
+        reducer_scratch(*groups["A"], arows, width),
     ]
     operands = (
         node_latent.reshape(nodes, width),
@@ -619,7 +682,6 @@
         scratch_shapes=[pltpu.VMEM(operand.shape, operand.dtype) for operand in operands]
         + [
             pltpu.VMEM((total // LANES, LANES, LANES), jnp.int16),
-            pltpu.VMEM((total // LANES, 16, LANES), jnp.int16),
             pltpu.VMEM((edges // LANES, LANES, LANES), jnp.int16),
             pltpu.VMEM((edges // LANES, LANES, LANES), jnp.int16),
             pltpu.VMEM(((total + nodes) // LANES, LANES, LANES), bf16),

time: 32.2 us -> 31.4 us (0.975)
  Pallas kernels: 31.3 us -> 30.5 us
    pallas_call x1, Pallas kernels: 30.1 us -> 29.2 us  [on_device(): pl.pallas_call(functools.partial(block_kernel, sizes, edge_scale, node_sc...]
where the time goes in v3:
time: 31.4 us; the launch traced here: 31.2 us
  Pallas kernels  30.5 us (97%)
  between operations  0.66 us (2%)
    pallas_call x1, Pallas kernels, on_device(): pl.pallas_call(functools.partial(block_kernel, sizes, edge_scale, node_sc...  29.2 us
    pallas_call x1, Pallas kernels, on_device(): pl.pallas_call(finish_kernel, out_shape=(shape(nodes, width), shape(edges...  1.27 us

profile of v3, /device:TPU:0, one launch (start us, length us, event | category | flops | bytes accessed | tf_op | source)
XLA Modules:
  0.0 31.2 jit_solution(7932271285360729742)
XLA Ops:
  0.7 29.2 %block_pass.1 = (f32[512,128]{1,0:T(8,128)S(1)}, bf16[2816,128]{1,0:T(8,128)(2,1)S(1)}, f32[512,128]{1,0:T(8,128)S(1)}, f32[448,128]{1,0:T(8,128)S(1)}, f32[256,...) custom-call(bf16[512,128]{1,0:T(8,128)(2,1)} %bitcast.18, ...), custom_call_target="tpu_custom_call" | custom-call | tf_op jit(solution)/shard_map/block_pass/pallas_call | solution.py:666
  29.9 1.3 %finish.1 = (f32[512,128]{1,0:T(8,128)}, bf16[2816,128]{1,0:T(8,128)(2,1)}, f32[384,128]{1,0:T(8,128)}, f32[2,128,128]{2,1,0:T(8,128)}, f32[3,128]{1,0:T(4,128)}...) custom-call(f32[512,128]{1,0:T(8,128)S(1)} %get-tuple-element.32.nod, ...), custom_call_target="tpu_custom_call" | custom-call | tf_op jit(solution)/shard_map/finish/pallas_call | solution.py:711

commit v4 on v3

--- a/solution.py
+++ b/solution.py
@@ -9,8 +9,8 @@
 
 EPSILON = 1e-05
 LANES = 128
-KINDS = {"N": "near", "B": "near", "A": "near"}
-PLAN = {"node": "N", "edge": "B", "scatter": "AN", "out1": "B", "out2": "A", "out3": "N", "late": "BAB", "end": "NA"}
+KINDS = {"N": "core", "B": "mix", "A": "cn"}
+PLAN = {"node": "N", "edge": "NB", "scatter": "A", "halo": "N", "out0": "AB", "out1": "ANB", "out2": "A", "late": "NBNB", "end": "A"}
 HALO = -1
 FORWARD_TILE = 768
 BACKWARD_TILE = 512
@@ -105,6 +105,7 @@
         "core": ([core, chips], [far], [chips, core]),
         "core2": ([core, chips], twice, [chips, core]),
         "mix": ([near], [far], [chips, core]),
+        "cn": ([core, chips], [far], [near]),
         "mix2": ([near], twice, [chips, core]),
     }
     return {name: kinds[kind] for name, kind in KINDS.items()}
@@ -129,12 +130,17 @@
     return index
 
 
+def hops(group, step):
+    far = [min(more, part[1] - more) for part, more in zip(group, step) if part[0] != "gz" or part[2] > 1]
+    return sum(far)
+
+
 def peers(group):
     steps = [()]
     for part in group:
         steps = [step + (more,) for step in steps for more in range(part[1])]
     found = []
-    for step in steps[1:]:
+    for step in sorted(steps[1:], key=lambda step: -hops(group, step)):
         index = 0
         device = {}
         for part, more in zip(group, step):
@@ -198,12 +204,12 @@
         self.scratch = self.scratch[4:]
         piece = self.now.shape[0] // group_size(group)
         for spot, (other, device) in enumerate(peers(group)):
-            rows = pl.ds(pl.multiple_of(other * piece, 8), piece)
+            rows = pl.ds(pl.multiple_of(other * piece, 2), piece)
             self.send(self.now.at[rows], landing.at[spot], device, spot, sems)
         self.count = group_size(group) - 1
         mine = member(group) * piece
         self.spot = self.spot + mine
-        self.arrived = landing, part, self.now.at[pl.ds(pl.multiple_of(mine, 8), piece)]
+        self.arrived = landing, part, self.now.at[pl.ds(pl.multiple_of(mine, 2), piece)]
 
     def swapped(self):
         self.wait()
@@ -230,14 +236,14 @@
     def settle(self, group):
         total = self.swapped()
         self.piece = self.now.shape[0]
-        self.out[pl.ds(pl.multiple_of(self.spot, 8), self.piece)] = total
+        self.out[pl.ds(pl.multiple_of(self.spot, 2), self.piece)] = total
         self.gather(group)
 
     def gather(self, group):
         self.wait()
         sems = self.scratch[:2]
         self.scratch = self.scratch[2:]
-        home = self.out.at[pl.ds(pl.multiple_of(self.spot, 8), self.piece)]
+        home = self.out.at[pl.ds(pl.multiple_of(self.spot, 2), self.piece)]
         for spot, (_, device) in enumerate(peers(group)):
             self.send(home, home, device, spot, sems)
         self.spot = self.spot - member(group) * self.piece
@@ -317,7 +323,7 @@
         pltpu.make_async_copy(source, target, loads.at[index])
         for index, (source, target) in enumerate(zip(sources, held))
     ]
-    order = [4, 3, 8, 0, 1, 2, 9, 10, 11, 12, 6, 13, 14, 15, 16, 7, 5]
+    order = [8, 10, 0, 1, 4, 3, 2, 9, 11, 12, 6, 13, 14, 15, 16, 7, 5]
     for index in order:
         loaded[index].start()
     arrive = lambda *which: [loaded[index].wait() for index in which]
@@ -337,12 +343,7 @@
     def column(row):
         return jnp.transpose(jnp.broadcast_to(row, (LANES, LANES)))
 
-    arrive(4, 3, 8, 0, 1, 2, 9, 10, 11, 12)
-    for block in range(edges // LANES):
-        at = slice(block * LANES, (block + 1) * LANES)
-        snd_col[block] = column(snd[:, at]).astype(jnp.int16)
-        rcv_col[block] = column(rcv[:, at]).astype(jnp.int16)
-
+    arrive(8, 0, 1, 10)
     def node_hots(ids, start, size, count):
         rows = [
             jnp.broadcast_to(ids[:, spot : spot + LANES], (LANES, LANES)).astype(jnp.int16)
@@ -380,15 +381,21 @@
     half = jnp.bfloat16(0.5)
     half_t = lambda weight: jnp.transpose(weight * half)
     w1 = [half_t(we1[index * width : (index + 1) * width]) for index in range(3)]
-    w2, w3 = half_t(weh[0]), jnp.transpose(weh[1])
-    back3, back2 = weh[1] * half, weh[0] * half
     bias = [column(0.5 * be[0:1]), column(0.5 * be[1:2]), column(be[2:3])]
-    gain, shift = column(ge[...]), column(se[...])
 
     put_blocks(table, 0, (matmul_nt(w1[1], node[...]) + wide(bias[0], nodes)).astype(bf16))
     put_blocks(table, nodes, (matmul_nt(w1[1], ghost[...]) + wide(bias[0], ghosts)).astype(bf16))
     put_blocks(table, total, matmul_nt(w1[2], node[...]).astype(bf16))
     spots = (total + nodes) // LANES
+
+    arrive(4, 3, 2, 9, 11, 12)
+    w2, w3 = half_t(weh[0]), jnp.transpose(weh[1])
+    back3, back2 = weh[1] * half, weh[0] * half
+    gain, shift = column(ge[...]), column(se[...])
+    for block in range(edges // LANES):
+        at = slice(block * LANES, (block + 1) * LANES)
+        snd_col[block] = column(snd[:, at]).astype(jnp.int16)
+        rcv_col[block] = column(rcv[:, at]).astype(jnp.int16)
 
     agg = [None]
 
@@ -438,7 +445,6 @@
     g1 = matmul(wnh[0] * half, r2) * slope1
     r1 = g1.astype(bf16)
     agg_grad = matmul(wn1[width:], r1).astype(bf16)
-    node_part = up + matmul(wn1[:width], r1)
     node_terms = [jnp.transpose(matmul(r1, node[...])), matmul_nt(agg, r1)]
     node_terms += [matmul_nt(z1, r2), matmul_nt(z2, r3)]
     for index, term in enumerate(node_terms):
@@ -447,17 +453,18 @@
         if pack.shape[0] > used:
             pack[used:] = jnp.zeros((pack.shape[0] - used, width), f32)
 
+    pl.semaphore_wait(barrier, len(greeted))
+    reach("node")
+
+    arrive(7)
+    node_part = up + matmul(wn1[:width], r1)
+
     def row_of(folded):
         return rows_sum(jnp.transpose(folded))
 
     node_sums = (lane_fold(g1), lane_fold(g2), lane_fold(g3), gain_sum)
     for index, value in enumerate(node_sums):
         bpack[3 * width + 5 + index : 3 * width + 6 + index] = row_of(value) * node_scale
-
-    pl.semaphore_wait(barrier, len(greeted))
-    reach("node")
-
-    arrive(7)
     small = [None] * 5
     grads = [None] * 3
     lefts = [agg_grad[:, spot : spot + LANES] for spot in range(0, nodes, LANES)]
@@ -624,8 +631,7 @@
     edge_scale = float(edges * devices) ** (-0.5)
     node_scale = float(nodes * devices) ** (-0.5)
 
-    def padded(rows, *groups):
-        unit = 8
+    def padded(rows, *groups, unit=8):
         for group in groups:
             unit *= group_size(group)
         return -(-rows // unit) * unit
@@ -635,7 +641,7 @@
 
     groups = set_groups(sizes)
     nrows = padded(4 * width, *groups["N"][0])
-    brows = padded(3 * width + 9, *groups["B"][0])
+    brows = padded(3 * width + 9, *groups["B"][0], unit=2)
     arows = padded(2 * width, *groups["A"][0])
     reducers = [
         reducer_scratch(*groups["N"], nrows, width),

time: 31.4 us -> 29.5 us (0.939)
  Pallas kernels: 30.5 us -> 28.7 us
    pallas_call x1, Pallas kernels: 29.2 us -> 27.5 us  [on_device(): pl.pallas_call(functools.partial(block_kernel, sizes, edge_scale, node_sc...]
where the time goes in v4:
time: 29.5 us; the launch traced here: 29.4 us
  Pallas kernels  28.7 us (97%)
  between operations  0.66 us (2%)
    pallas_call x1, Pallas kernels, on_device(): pl.pallas_call(functools.partial(block_kernel, sizes, edge_scale, node_sc...  27.5 us
    pallas_call x1, Pallas kernels, on_device(): pl.pallas_call(finish_kernel, out_shape=(shape(nodes, width), shape(edges...  1.27 us

profile of v4, /device:TPU:0, one launch (start us, length us, event | category | flops | bytes accessed | tf_op | source)
XLA Modules:
  0.0 29.4 jit_solution(10623203554303803946)
XLA Ops:
  0.7 27.5 %block_pass.1 = (f32[512,128]{1,0:T(8,128)S(1)}, bf16[2816,128]{1,0:T(8,128)(2,1)S(1)}, f32[512,128]{1,0:T(8,128)S(1)}, f32[400,128]{1,0:T(8,128)S(1)}, f32[256,...) custom-call(bf16[512,128]{1,0:T(8,128)(2,1)} %bitcast.18, ...), custom_call_target="tpu_custom_call" | custom-call | tf_op jit(solution)/shard_map/block_pass/pallas_call | solution.py:672
  28.1 1.3 %finish.1 = (f32[512,128]{1,0:T(8,128)}, bf16[2816,128]{1,0:T(8,128)(2,1)}, f32[384,128]{1,0:T(8,128)}, f32[2,128,128]{2,1,0:T(8,128)}, f32[3,128]{1,0:T(4,128)}...) custom-call(f32[512,128]{1,0:T(8,128)S(1)} %get-tuple-element.32.nod, ...), custom_call_target="tpu_custom_call" | custom-call | tf_op jit(solution)/shard_map/finish/pallas_call | solution.py:717

commit v5 on v4

--- a/solution.py
+++ b/solution.py
@@ -13,7 +13,7 @@
 PLAN = {"node": "N", "edge": "NB", "scatter": "A", "halo": "N", "out0": "AB", "out1": "ANB", "out2": "A", "late": "NBNB", "end": "A"}
 HALO = -1
 FORWARD_TILE = 768
-BACKWARD_TILE = 512
+BACKWARD_TILE = 768
 MESH = pl.DeviceIdType.MESH
 AXES = ("gx", "gy", "gz")
 

time: 29.5 us -> 29.6 us (level)
  no operation moved by 1% of the time
where the time goes in v5:
time: 29.6 us; the launch traced here: 29.4 us
  Pallas kernels  28.8 us (97%)
  between operations  0.66 us (2%)
    pallas_call x1, Pallas kernels, on_device(): pl.pallas_call(functools.partial(block_kernel, sizes, edge_scale, node_sc...  27.5 us
    pallas_call x1, Pallas kernels, on_device(): pl.pallas_call(finish_kernel, out_shape=(shape(nodes, width), shape(edges...  1.27 us

profile of v5, /device:TPU:0, one launch (start us, length us, event | category | flops | bytes accessed | tf_op | source)
XLA Modules:
  0.0 29.4 jit_solution(13568276344781787123)
XLA Ops:
  0.7 27.5 %block_pass.1 = (f32[512,128]{1,0:T(8,128)S(1)}, bf16[2816,128]{1,0:T(8,128)(2,1)S(1)}, f32[512,128]{1,0:T(8,128)S(1)}, f32[400,128]{1,0:T(8,128)S(1)}, f32[256,...) custom-call(bf16[512,128]{1,0:T(8,128)(2,1)} %bitcast.18, ...), custom_call_target="tpu_custom_call" | custom-call | tf_op jit(solution)/shard_map/block_pass/pallas_call | solution.py:672
  28.2 1.3 %finish.1 = (f32[512,128]{1,0:T(8,128)}, bf16[2816,128]{1,0:T(8,128)(2,1)}, f32[384,128]{1,0:T(8,128)}, f32[2,128,128]{2,1,0:T(8,128)}, f32[3,128]{1,0:T(4,128)}...) custom-call(f32[512,128]{1,0:T(8,128)S(1)} %get-tuple-element.32.nod, ...), custom_call_target="tpu_custom_call" | custom-call | tf_op jit(solution)/shard_map/finish/pallas_call | solution.py:717
